TPU v7x, 32 devices: a whole 2x2x4 slice. The times are simulated.
32 devices in a mesh: site: 2 (over y), handler: 4 (over x, core), worker: 4 (over z).
Axes of the slice: x: 2, y: 2, z: 4, core: 2. Of those that a mesh axis runs over, the one named last changes fastest.
Arguments:
- sgt: bfloat16 [2048, 6, 3, 1024], P(('site', 'handler', 'worker')), parts along dimension 0, may hold values from -6 to 6
- mechanism: bfloat16 [6, 1024], P(None, ('handler', 'worker')), may hold values from -2.5 to 2.5
- req_owner: int32 [1024, 1], P(('site', 'handler', 'worker')), parts along dimension 0, may hold values from 0 to 15; in each aligned block of 32 rows (0 to 31, 32 to 63, ...) at most 4 rows name the same one
- req_local: int32 [1024], P(('site', 'handler', 'worker')), parts along dimension 0, may hold values from 0 to 31
- slip: bfloat16 [1024, 64, 128], P(('site', 'handler', 'worker')), parts along dimension 0, may hold values from 0 to 0.029907227
Outputs:
- seismograms: float32 [32, 64, 3, 1024], P(('site', 'handler'), 'worker'), parts along dimension 0
There are 2 independent parts, one for each index of `site`. A program takes and returns all parts, laid end to end along the dimension named above; an argument that names none is the same for every part. Nothing has to cross between parts.
Inputs may be any that keep to these rules, and one draw needn't show every extreme that they name: `req_owner`: among the 32 requests of one device no owner is named more than 4 times, and in every draw some device names some owner exactly 4 times; every owner is named somewhere.
All inputs are finite; a program needn't handle non-finite values.
Results may differ from a plain program's by a relative error of at most 0.0029.
Values may be sent and summed in bfloat16 or wider, within the bound.
No kernel may reach another device: no remote copies, remote signals or barrier semaphores. Data moves between devices by JAX's collectives and lax.ppermute only.
A program may use at most 128 MiB of HBM per device.

v0:
```python
import functools

import jax
import jax.numpy as jnp
from jax import lax
from jax.experimental import pallas as pl
from jax.experimental.pallas import tpu as pltpu
from jax.sharding import PartitionSpec as P


TAPS = 64
BLK = 2
RUP_SLOTS = 4
LANES = 128
SUB = 8
PARTS = 2
VMEM_BUDGET = 12 * 1024 * 1024
MIB = 1024 * 1024
BF = jnp.bfloat16
F32 = jnp.float32


def combine_points(sgt, mechanism):
    total = mechanism[0].astype(jnp.float32)[:, None, None] * sgt[:, 0].astype(jnp.float32)
    for comp in range(1, 6):
        total = total + mechanism[comp].astype(jnp.float32)[:, None, None] * sgt[:, comp].astype(
            jnp.float32
        )
    return total.astype(jnp.bfloat16)


def shifted_blocks(green):
    samples = green.shape[-1]
    padded = jnp.pad(green, ((0, 0), (0, 0), (0, 0), (TAPS, 0)))
    return jnp.stack(
        [padded[..., TAPS - lag : TAPS - lag + samples] for lag in range(TAPS)], axis=2
    )


def deliver(first, second):
    return (
        lax.all_to_all(first, ("handler", "worker"), split_axis=0, concat_axis=0, tiled=True),
        lax.all_to_all(second, ("handler", "worker"), split_axis=0, concat_axis=0, tiled=True),
    )


def local_exchange(sgt, mechanism, req_owner, req_local, slip):
    peers = lax.axis_size(("handler", "worker"))
    samples = sgt.shape[-1]
    blocks_here = sgt.shape[0] // BLK
    requests = req_local.shape[0]
    capacity = max(2, (2 * requests + peers - 1) // peers)
    owner = req_owner[:, 0]
    member = (owner[:, None] == jnp.arange(peers, dtype=jnp.int32)[None, :]).astype(jnp.int32)
    earlier = jnp.sum((jnp.cumsum(member, axis=0) - member) * member, axis=1)
    position = owner * capacity + earlier
    table = jnp.full((peers * capacity,), -1, jnp.int32).at[position].set(req_local)
    asked = lax.all_to_all(
        table.reshape(peers, capacity),
        ("handler", "worker"),
        split_axis=0,
        concat_axis=0,
        tiled=True,
    )
    wanted = (asked >= 0).reshape(-1)
    picked = jnp.where(wanted, asked.reshape(-1), 0)
    green_here = combine_points(sgt, mechanism).reshape(blocks_here, BLK, 3, samples)
    chosen = jnp.where(wanted[:, None, None, None], green_here[picked], jnp.zeros((), jnp.bfloat16))
    chosen = chosen.reshape(peers, capacity, BLK, 3, samples)
    front, back = deliver(chosen[:, :, :, :2], chosen[:, :, :, 2:])
    arrived = jnp.concatenate([front, back], axis=3)
    blocks = arrived.reshape(peers * capacity, BLK, 3, samples)[position]
    rows = requests // RUP_SLOTS
    variations = slip.shape[1]
    outputs = []
    for slot in range(RUP_SLOTS):
        stacked = shifted_blocks(blocks[slot * rows : (slot + 1) * rows])
        right = stacked.reshape(rows * BLK * TAPS, 3 * samples)
        left = jnp.transpose(slip[slot * rows : (slot + 1) * rows], (1, 0, 2)).reshape(
            variations, rows * BLK * TAPS
        )
        outputs.append(
            jnp.dot(left, right, preferred_element_type=jnp.float32).reshape(variations, 3, samples)
        )
    partial_value = jnp.stack(outputs, axis=0)
    return lax.psum_scatter(partial_value, "worker", scatter_dimension=1, tiled=True)


def combine_kernel(samples, sgt_ref, mech_ref, same_ref, other_ref, mech_scratch):
    step = pl.program_id(0)
    count = same_ref.shape[0]

    @pl.when(step == 0)
    def _():
        mech_scratch[...] = jnp.transpose(mech_ref[...].astype(F32))

    mech = mech_scratch[pl.ds(pl.multiple_of(step * count, count), count), :]
    green = []
    for k in range(3):
        total = mech[:, 0:1] * sgt_ref[0, k].astype(F32)
        for comp in range(1, 6):
            total = total + mech[:, comp : comp + 1] * sgt_ref[comp, k].astype(F32)
        green.append(total.astype(BF))
    half = samples // 2
    parity = lax.rem(lax.axis_index("worker"), 2)

    def write(low_ref, high_ref):
        low_ref[:, :samples] = green[0]
        low_ref[:, samples : samples + LANES] = jnp.zeros((count, LANES), BF)
        low_ref[:, samples + LANES :] = green[1][:, :half]
        high_ref[:, :samples] = green[2]
        high_ref[:, samples:] = green[1][:, half - LANES :]

    @pl.when(parity == 0)
    def _():
        write(same_ref, other_ref)

    @pl.when(parity == 1)
    def _():
        write(other_ref, same_ref)


def combine(sgt, mechanism):
    points, comps, kinds, samples = sgt.shape
    width = samples + LANES + samples // 2
    step = min(16, points)
    out = jax.ShapeDtypeStruct((points, width), BF)
    return pl.pallas_call(
        functools.partial(combine_kernel, samples),
        grid=(points // step,),
        in_specs=[
            pl.BlockSpec((comps, kinds, step, samples), lambda p: (0, 0, p, 0)),
            pl.BlockSpec((comps, points), lambda p: (0, 0)),
        ],
        out_specs=[pl.BlockSpec((step, width), lambda p: (p, 0))] * 2,
        out_shape=[out, out],
        scratch_shapes=[pltpu.VMEM((points, comps), F32)],
        compiler_params=pltpu.CompilerParams(vmem_limit_bytes=16 * MIB),
        name="combine",
    )(jnp.transpose(sgt, (1, 2, 0, 3)), mechanism)


def group_transpose(rows, lane):
    rows = list(rows)
    count = len(rows)
    step = count // 2
    while step:
        keep = (lane // (SUB * step)) % 2 == 0
        for j in range(count):
            if j & step:
                continue
            low, high = rows[j], rows[j + step]
            rows[j] = jnp.where(keep, low, pltpu.roll(high, SUB * step, 1))
            rows[j + step] = jnp.where(keep, pltpu.roll(low, LANES - SUB * step, 1), high)
        step //= 2
    return rows


def turn_kernel(slip_ref, own_ref, *rest):
    others, grouped = rest[:-1], rest[-1]
    slots, coarse, group, _ = own_ref.shape
    rows = slip_ref.shape[0] // slots
    mine = lax.axis_index("worker") // 2
    tall = 2 * SUB
    lane = lax.broadcasted_iota(jnp.int32, (tall, LANES), 1)
    source = lax.broadcasted_iota(jnp.int32, (LANES, LANES), 0)
    target = lax.broadcasted_iota(jnp.int32, (LANES, LANES), 1)
    fine, row, point = source % SUB, (source % TAPS) // SUB, source // TAPS
    place = jnp.where(target == (fine * rows + row) * BLK + point, 1.0, 0.0).astype(BF)

    def turn(out, g, first, slot):
        for v in range(0, group, tall):
            at = pl.multiple_of((mine ^ g) * group + v, tall)
            turned = group_transpose(
                [slip_ref[(first + slot) * rows + n, pl.ds(at, tall), :] for n in range(rows)], lane
            )
            for a in range(coarse):
                grouped[a * group + v : a * group + v + tall, :] = turned[a]
        moved = jnp.dot(grouped[...], place, preferred_element_type=F32).astype(BF)
        for a in range(coarse):
            out[slot, a] = moved[a * group : (a + 1) * group]

    for index, out in enumerate(others):
        g, part = divmod(index, PARTS)
        first = part * out.shape[0]

        @pl.loop(0, out.shape[0])
        def _(slot, out=out, g=g, first=first):
            turn(out, g + 1, first, slot)

    @pl.loop(0, slots)
    def _(slot):
        turn(own_ref, 0, 0, slot)


def turn_slip(slip, workers):
    _, variations, depth = slip.shape
    groups = workers // 2
    group = variations // groups
    whole = jax.ShapeDtypeStruct((RUP_SLOTS, TAPS // SUB, group, depth), BF)
    piece = jax.ShapeDtypeStruct((RUP_SLOTS // PARTS, TAPS // SUB, group, depth), BF)
    outs = [whole] + [piece] * ((groups - 1) * PARTS)
    vmem = pl.BlockSpec(memory_space=pltpu.VMEM)
    return pl.pallas_call(
        turn_kernel,
        in_specs=[vmem],
        out_specs=[vmem] * len(outs),
        out_shape=outs,
        scratch_shapes=[pltpu.VMEM((TAPS // SUB * group, depth), BF)],
        compiler_params=pltpu.CompilerParams(vmem_limit_bytes=8 * MIB),
        name="turn_slip",
    )(slip)


def gather_kernel(rows_ref, *refs):
    green, dense, hot = refs[:-2], refs[-2], refs[-1]
    pieces = len(green)
    points, width = green[0].shape
    span = 2 * LANES
    asked = rows_ref[...]
    for c in range(0, pieces * points, LANES):
        column = lax.broadcasted_iota(jnp.int32, (asked.shape[0], LANES), 1) + c
        hot[:, c : c + LANES] = jnp.where(asked == column, 1.0, 0.0).astype(BF)
    together = max(1, span // points)
    for c in range(0, width, span):
        e = min(width, c + span)
        total = None
        for p in range(0, pieces, together):
            block = jnp.concatenate([g[:, c:e] for g in green[p : p + together]], axis=0)
            part = jnp.dot(
                hot[:, p * points : (p + together) * points], block, preferred_element_type=F32
            )
            total = part if total is None else total + part
        dense[:, c:e] = total.astype(BF)


def gather(rows, green):
    points, width = green[0].shape
    vmem = pl.BlockSpec(memory_space=pltpu.VMEM)
    return pl.pallas_call(
        gather_kernel,
        in_specs=[vmem] * (1 + len(green)),
        out_specs=vmem,
        out_shape=jax.ShapeDtypeStruct((rows.shape[0], width), BF),
        scratch_shapes=[pltpu.VMEM((rows.shape[0], len(green) * points), BF)],
        compiler_params=pltpu.CompilerParams(vmem_limit_bytes=8 * MIB),
        name="gather",
    )(rows, *green)


def convolve_kernel(base, dense, *refs):
    slips = refs[:-5]
    own_ref, send_ref, left, right, product = refs[-5:]
    sources = len(slips)
    width = dense.shape[1]
    slots = own_ref.shape[0]
    _, coarse, group, _ = slips[0].shape
    per_source = dense.shape[0] // (RUP_SLOTS * sources)
    tiles = width // LANES
    samples = (width - LANES) * 2 // 3
    first = samples // LANES
    parity = lax.rem(lax.axis_index("worker"), 2)
    span = 2 * LANES
    lane = lax.broadcasted_iota(jnp.int32, (SUB, LANES), 1)
    wide_lane = lax.broadcasted_iota(jnp.int32, (per_source, LANES), 1)
    zero = jnp.zeros((SUB, LANES), F32)

    def slot_body(slot, carry):
        for j in range(sources):
            for a in range(coarse):
                left[a * group : (a + 1) * group, j * LANES : (j + 1) * LANES] = slips[j][
                    slot + (base if slips[j].shape[0] > slots else 0), a
                ]
            at = pl.multiple_of(((base + slot) * sources + j) * per_source, per_source)
            for b in range(SUB):
                put = j * LANES + b * per_source
                before = jnp.zeros((per_source, LANES), BF)
                for m in range(tiles):
                    value = dense[pl.ds(at, per_source), m * LANES : (m + 1) * LANES]
                    if b:
                        turn = pltpu.roll(value, b, 1)
                        if m == first:
                            before = jnp.zeros((per_source, LANES), BF)
                        value = jnp.where(wide_lane < b, before, turn)
                        before = turn
                    right[put : put + per_source, m * LANES : (m + 1) * LANES] = value

        for c in range(0, width, span):
            e = min(width, c + span)
            product[:, c:e] = jnp.dot(left[...], right[:, c:e], preferred_element_type=F32)

        for side in range(2):
            for u in range(0, group // 2, SUB):
                total = [None] * tiles
                for a in range(coarse):
                    start = pl.multiple_of(
                        a * group + lax.rem(parity + side, 2) * (group // 2) + u, SUB
                    )
                    before = zero
                    for m in range(tiles):
                        value = product[pl.ds(start, SUB), m * LANES : (m + 1) * LANES]
                        if a:
                            value = pltpu.roll(value, a * SUB, 1)
                        if m == first:
                            before = zero
                        moved = jnp.where(lane < a * SUB, before, value) if a else value
                        before = value
                        total[m] = moved if total[m] is None else total[m] + moved
                total = total[:first] + total[first + 1 :]
                for m, value in enumerate(total):
                    if side == 0:
                        own_ref[slot, u : u + SUB, m * LANES : (m + 1) * LANES] = value
                    else:
                        send_ref[slot, u : u + SUB, m * LANES : (m + 1) * LANES] = value.astype(BF)
        return carry

    lax.fori_loop(0, slots, slot_body, 0)


def convolve(base, dense, slips):
    width = dense.shape[1]
    slots = slips[-1].shape[0]
    _, coarse, group, depth = slips[0].shape
    inner = depth * len(slips)
    vmem = pl.BlockSpec(memory_space=pltpu.VMEM)
    return pl.pallas_call(
        functools.partial(convolve_kernel, base),
        in_specs=[vmem] * (1 + len(slips)),
        out_specs=[vmem, vmem],
        out_shape=[
            jax.ShapeDtypeStruct((slots, group // 2, width - LANES), F32),
            jax.ShapeDtypeStruct((slots, group // 2, width - LANES), BF),
        ],
        scratch_shapes=[
            pltpu.VMEM((coarse * group, inner), BF),
            pltpu.VMEM((inner, width), BF),
            pltpu.VMEM((coarse * group, width), F32),
        ],
        compiler_params=pltpu.CompilerParams(vmem_limit_bytes=12 * MIB),
        name="convolve",
    )(dense, *slips)


def assemble_kernel(own_ref, got_ref, *refs):
    out_ref = refs[-1]
    _, _, _, samples = out_ref.shape
    half = samples // 2
    parity = lax.rem(lax.axis_index("worker"), 2)

    def write(low, high):
        out_ref[0, 0] = low[0, :, :samples].astype(F32)
        out_ref[0, 1, :, :half] = low[0, :, samples:].astype(F32)
        out_ref[0, 1, :, half:] = high[0, :, samples:].astype(F32)
        out_ref[0, 2] = high[0, :, :samples].astype(F32)

    @pl.when(parity == 0)
    def _():
        write(own_ref, got_ref)

    @pl.when(parity == 1)
    def _():
        write(got_ref, own_ref)


def assemble(base, own, got, samples, into):
    slots, group, width = own.shape
    spec = pl.BlockSpec((1, group, width), lambda r: (r, 0, 0))
    more = () if into is None else (into,)
    return pl.pallas_call(
        assemble_kernel,
        grid=(slots,),
        in_specs=[spec, spec] + [pl.BlockSpec(memory_space=pl.ANY)] * len(more),
        out_specs=pl.BlockSpec((1, 3, group, samples), lambda r: (base + r, 0, 0, 0)),
        out_shape=jax.ShapeDtypeStruct((RUP_SLOTS, 3, group, samples), F32),
        input_output_aliases={2: 0} if more else {},
        compiler_params=pltpu.CompilerParams(vmem_limit_bytes=8 * MIB),
        name="assemble",
    )(own, got, *more)


def swap(value, axis, flip):
    return lax.ppermute(value, axis, [(i, i ^ flip) for i in range(lax.axis_size(axis))])


def local_replicate(sgt, mechanism, req_owner, req_local, slip):
    handlers, workers = lax.axis_size("handler"), lax.axis_size("worker")
    handler, worker = lax.axis_index("handler"), lax.axis_index("worker")
    points, _, _, samples = sgt.shape
    blocks_here = points // BLK
    requests = req_local.shape[0]
    same, other = combine(sgt, mechanism)

    code = req_owner[:, 0] * blocks_here + req_local
    codes = jnp.stack([code] + [swap(code, "worker", flip) for flip in range(1, workers)])
    owner = codes // blocks_here
    piece = ((owner // workers) ^ handler) * workers + ((owner % workers) ^ worker)
    row = piece * points + codes % blocks_here * BLK
    row = jnp.transpose(row.reshape(workers, RUP_SLOTS, requests // RUP_SLOTS), (1, 0, 2))
    rows = (row[..., None] + jnp.arange(BLK, dtype=jnp.int32)).reshape(-1, 1)

    green = {(0, 0): same}
    for flip in range(1, workers):
        green[0, flip] = swap(other if flip % 2 else same, "worker", flip)
    green[0, workers - 1], rows = lax.optimization_barrier((green[0, workers - 1], rows))
    bit = handlers // 2
    while bit:
        for (hand, flip), value in list(green.items()):
            green[hand ^ bit, flip] = swap(value, "handler", bit)
        bit //= 2
    dense = gather(rows, [green[hand, flip] for hand in range(handlers) for flip in range(workers)])

    turned = turn_slip(slip, workers)
    near = [turned[0], swap(turned[0], "worker", 1)]
    out = None
    results = []
    for part in range(PARTS):
        slips = list(near)
        for flip in range(2, workers, 2):
            value = turned[1 + (flip // 2 - 1) * PARTS + part]
            slips.append(swap(value, "worker", flip))
            slips.append(swap(slips[-1], "worker", 1))
        own, send = convolve(part * RUP_SLOTS // PARTS, dense, slips)
        results.append((own, swap(send, "worker", 1)))
    for part, (own, got) in enumerate(results):
        out = assemble(part * RUP_SLOTS // PARTS, own, got, samples, out)
    return jnp.transpose(out, (0, 2, 1, 3))


def power_of_two(count):
    return count & (count - 1) == 0


def replicated(handlers, workers, points, kinds, samples, requests, variations, depth):
    width = samples + samples // 2 + LANES
    return (
        handlers * workers * points * width * 4 <= VMEM_BUDGET
        and power_of_two(handlers)
        and power_of_two(workers)
        and workers >= 2
        and kinds == 3
        and samples % (2 * LANES) == 0
        and depth == BLK * TAPS == LANES
        and requests // RUP_SLOTS == TAPS // SUB
        and variations % (workers * SUB) == 0
    )


def solution(mesh):
    handlers, workers = mesh.shape["handler"], mesh.shape["worker"]

    def local(sgt, mechanism, req_owner, req_local, slip):
        points, _, kinds, samples = sgt.shape
        requests, variations, depth = slip.shape
        if replicated(handlers, workers, points, kinds, samples, requests, variations, depth):
            return local_replicate(sgt, mechanism, req_owner, req_local, slip)
        return local_exchange(sgt, mechanism, req_owner, req_local, slip)

    return jax.shard_map(
        local,
        mesh=mesh,
        in_specs=(
            P(("site", "handler", "worker"), None, None, None),
            P(None, ("handler", "worker")),
            P(("site", "handler", "worker"), None),
            P(("site", "handler", "worker")),
            P(("site", "handler", "worker"), None, None),
        ),
        out_specs=P(("site", "handler"), "worker", None, None),
        check_vma=False,
    )
```

profile of v0, /device:TPU:0, one launch (start us, length us, event | category | flops | bytes accessed | tf_op | source)
XLA Modules:
  0.0 72.9 jit_solution(7220295168529088615)
XLA Ops:
  0.0 0.7 bitcast_add_fusion
  0.7 5.1 %collective-permute-start.3 = (s32[32]{0:T(128)S(1)}, s32[32]{0:T(128)S(1)}, u32[]{:S(2)}, u32[]{:S(2)}) collective-permute-start(s32[32]{0:T(128)S(1)} %bitcast_add_fusion), channel_id=1, source_target_pairs={{0,3},{1,2},{2,1},{3,0},{4,7},{5,6},{6,5},{7,4},{8,11},{9,10},{10,... | collective-permute-start | bytes 392 | tf_op jit(solution)/shard_map/ppermute | solution.py:382
  5.8 0.0 collective-permute-start.2
  5.8 0.6 collective-permute-start.1
  6.3 1.7 %copy-done = bf16[64,6,3,1024]{3,0,2,1:T(8,128)(2,1)S(1)} copy-done((bf16[64,6,3,1024]{3,0,2,1:T(8,128)(2,1)S(1)}, bf16[64,6,3,1024]{3,0,2,1:T(8,128)(2,1)}, u32[]{:S(2)}) %copy-start) | copy-done | bytes 2359320
  8.0 0.7 copy-done.4
  8.7 1.1 %combine.1 = (bf16[64,1664]{1,0:T(8,128)(2,1)S(1)}, bf16[64,1664]{1,0:T(8,128)(2,1)S(1)}) custom-call(bf16[6,3,64,1024]{3,2,1,0:T(8,128)(2,1)S(1)} %bitcast.8, bf16[6,64]{1,0:T(8,128)(2,1)S(1)} %copy-done.4), custom_call_target="tpu_custom_call" | custom-call | tf_op jit(solution)/shard_map/combine/pallas_call | solution.py:128
  9.8 1.5 %collective-permute-start.4 = (bf16[64,1664]{1,0:T(8,128)(2,1)S(1)}, bf16[64,1664]{1,0:T(8,128)(2,1)S(1)}, u32[]{:S(2)}, u32[]{:S(2)}) collective-permute-start(bf16[64,1664]{1,0:T(8,128)(2,1)S(1)} %get-tuple-element.16), channel_id=1, source_target_pairs={{0,1},{1,0},{2,3},{3,2},{4,5},{5,4},{6,7},{7,6},{8,9},{9,8},{10,11... | collective-permute-start | bytes 638984 | tf_op jit(solution)/shard_map/ppermute | solution.py:382
  11.3 2.4 %collective-permute-start = (bf16[64,1664]{1,0:T(8,128)(2,1)S(1)}, bf16[64,1664]{1,0:T(8,128)(2,1)S(1)}, u32[]{:S(2)}, u32[]{:S(2)}) collective-permute-start(bf16[64,1664]{1,0:T(8,128)(2,1)S(1)} %get-tuple-element.16), channel_id=1, source_target_pairs={{0,3},{1,2},{2,1},{3,0},{4,7},{5,6},{6,5},{7,4},{8,11},{9,10},{10,... | collective-permute-start | bytes 638984 | tf_op jit(solution)/shard_map/ppermute | solution.py:382
  13.7 0.1 stack.15
  13.8 2.9 %turn_slip.1 = (bf16[4,8,32,128]{3,2,1,0:T(8,128)(2,1)S(1)}, bf16[2,8,32,128]{3,2,1,0:T(8,128)(2,1)S(1)}, bf16[2,8,32,128]{3,2,1,0:T(8,128)(2,1)S(1)}) custom-call(bf16[32,64,128]{2,1,0:T(8,128)(2,1)S(1)} %copy-done.1), custom_call_target="tpu_custom_call" | custom-call | tf_op jit(solution)/shard_map/turn_slip/pallas_call | solution.py:204
  16.7 0.0 collective-permute-done.1
  16.7 1.6 %collective-permute-start.10 = (bf16[64,1664]{1,0:T(8,128)(2,1)S(1)}, bf16[64,1664]{1,0:T(8,128)(2,1)S(1)}, u32[]{:S(2)}, u32[]{:S(2)}) collective-permute-start(bf16[64,1664]{1,0:T(8,128)(2,1)S(1)} %get-tuple-element.18.refs_0_), channel_id=1, source_target_pairs={{0,8},{4,12},{8,0},{12,4},{1,9},{5,13},{9,1},{13,5},{2,10},{6,14},... | collective-permute-start | bytes 638984 | tf_op jit(solution)/shard_map/ppermute | solution.py:382
  18.3 0.1 stack.16
  18.4 0.0 collective-permute-done.2
  18.4 0.5 collective-permute-start.19
  18.9 0.1 stack.17
  19.0 0.0 collective-permute-done.3
  19.0 2.5 %collective-permute-start.22 = (bf16[2,8,32,128]{3,2,1,0:T(8,128)(2,1)S(1)}, bf16[2,8,32,128]{3,2,1,0:T(8,128)(2,1)}, u32[]{:S(2)}, u32[]{:S(2)}) collective-permute-start(bf16[2,8,32,128]{3,2,1,0:T(8,128)(2,1)S(1)} %get-tuple-element.24), channel_id=1, source_target_pairs={{0,2},{1,3},{2,0},{3,1},{4,6},{5,7},{6,4},{7,5},{8,10},{9,11},{10,... | collective-permute-start | bytes 393224 | tf_op jit(solution)/shard_map/ppermute | solution.py:382
  21.5 0.1 stack.18
  21.7 9.9 %collective-permute-done.19.refs_2_ = bf16[2,8,32,128]{3,2,1,0:T(8,128)(2,1)S(1)} collective-permute-done((bf16[2,8,32,128]{3,2,1,0:T(8,128)(2,1)S(1)}, bf16[2,8,32,128]{3,2,1,0:T(8,128)(2,1)S(1)}, u32[]{:S(2)}, u32[]{:S(2)}) %collective-permute-start.19) | collective-permute-done | bytes 131104 | tf_op jit(solution)/shard_map/ppermute | solution.py:382
  31.5 0.0 collective-permute-start.6
  31.5 2.7 %collective-permute-done.22.refs_2_ = bf16[2,8,32,128]{3,2,1,0:T(8,128)(2,1)} collective-permute-done((bf16[2,8,32,128]{3,2,1,0:T(8,128)(2,1)S(1)}, bf16[2,8,32,128]{3,2,1,0:T(8,128)(2,1)}, u32[]{:S(2)}, u32[]{:S(2)}) %collective-permute-start.22) | collective-permute-done | bytes 131104 | tf_op jit(solution)/shard_map/ppermute | solution.py:382
  34.2 0.0 collective-permute-start.5
  34.2 0.0 collective-permute-done.4.refs_1_
  34.3 1.5 %collective-permute-start.11 = (bf16[64,1664]{1,0:T(8,128)(2,1)S(1)}, bf16[64,1664]{1,0:T(8,128)(2,1)S(1)}, u32[]{:S(2)}, u32[]{:S(2)}) collective-permute-start(bf16[64,1664]{1,0:T(8,128)(2,1)S(1)} %collective-permute-done.4.refs_1_), channel_id=1, source_target_pairs={{0,8},{4,12},{8,0},{12,4},{1,9},{5,13},{9,1},{13,5},{2,10},{6,14},... | collective-permute-start | bytes 638984 | tf_op jit(solution)/shard_map/ppermute | solution.py:382
  35.7 0.1 iota_add_fusion
  35.8 0.7 add.58
  36.5 0.0 collective-permute-done.refs_3_
  36.6 0.0 collective-permute-start.7
  36.6 0.0 collective-permute-done.10.refs_8_
  36.6 0.6 collective-permute-start.13
  37.2 0.0 collective-permute-done.6.refs_4_
  37.2 0.2 collective-permute-start.9
  37.3 8.5 %collective-permute-done.5.refs_2_ = bf16[64,1664]{1,0:T(8,128)(2,1)S(1)} collective-permute-done((bf16[64,1664]{1,0:T(8,128)(2,1)S(1)}, bf16[64,1664]{1,0:T(8,128)(2,1)S(1)}, u32[]{:S(2)}, u32[]{:S(2)}) %collective-permute-start.5) | collective-permute-done | bytes 213024 | tf_op jit(solution)/shard_map/ppermute | solution.py:382
  45.8 0.0 collective-permute-start.14
  45.8 0.0 collective-permute-done.11.refs_9_
  45.9 1.5 %collective-permute-start.12 = (bf16[64,1664]{1,0:T(8,128)(2,1)S(1)}, bf16[64,1664]{1,0:T(8,128)(2,1)S(1)}, u32[]{:S(2)}, u32[]{:S(2)}) collective-permute-start(bf16[64,1664]{1,0:T(8,128)(2,1)S(1)} %collective-permute-done.5.refs_2_), channel_id=1, source_target_pairs={{0,8},{4,12},{8,0},{12,4},{1,9},{5,13},{9,1},{13,5},{2,10},{6,14},... | collective-permute-start | bytes 638984 | tf_op jit(solution)/shard_map/ppermute | solution.py:382
  47.4 0.0 collective-permute-done.7.refs_5_
  47.4 0.2 collective-permute-start.8
  47.6 0.0 collective-permute-done.13.refs_11_
  47.6 0.3 collective-permute-start.15
  47.9 0.0 collective-permute-done.9.refs_7_
  47.9 0.3 collective-permute-start.17
  48.2 5.3 %collective-permute-done.12.refs_10_ = bf16[64,1664]{1,0:T(8,128)(2,1)S(1)} collective-permute-done((bf16[64,1664]{1,0:T(8,128)(2,1)S(1)}, bf16[64,1664]{1,0:T(8,128)(2,1)S(1)}, u32[]{:S(2)}, u32[]{:S(2)}) %collective-permute-start.12) | collective-permute-done | bytes 213024 | tf_op jit(solution)/shard_map/ppermute | solution.py:382
  53.5 0.0 copy-start.2
  53.5 0.7 copy-done.2
  54.2 2.0 %collective-permute-start.20 = (bf16[2,8,32,128]{3,2,1,0:T(8,128)(2,1)S(1)}, bf16[2,8,32,128]{3,2,1,0:T(8,128)(2,1)}, u32[]{:S(2)}, u32[]{:S(2)}) collective-permute-start(bf16[2,8,32,128]{3,2,1,0:T(8,128)(2,1)S(1)} %collective-permute-done.19.refs_2_), channel_id=1, source_target_pairs={{0,1},{1,0},{2,3},{3,2},{4,5},{5,4},{6,7},{7,6},{8,9},{9,8},{10,11... | collective-permute-start | bytes 393224 | tf_op jit(solution)/shard_map/ppermute | solution.py:382
  56.2 0.8 %copy.9.rows_ref = s32[256,1]{1,0:T(8,128)S(1)} copy(s32[256,1]{0,1:T(1,128)} %add.58) | data formatting | bytes 2048 | tf_op jit(solution)/shard_map/optimization_barrier | solution.py:404
  57.0 0.0 collective-permute-done.16.refs_14_
  57.0 0.0 copy-start.3
  57.1 0.9 %copy-done.3 = bf16[64,1664]{1,0:T(8,128)(2,1)S(1)} copy-done((bf16[64,1664]{1,0:T(8,128)(2,1)S(1)}, bf16[64,1664]{1,0:T(8,128)(2,1)}, u32[]{:S(2)}) %copy-start.3) | copy-done | bytes 213016
  58.0 2.2 %gather.1.dense = bf16[256,1664]{1,0:T(8,128)(2,1)S(1)} custom-call(s32[256,1]{1,0:T(8,128)S(1)} %copy.9.rows_ref, bf16[64,1664]{1,0:T(8,128)(2,1)S(1)} %get-tuple-element.18.refs_0_, bf16[64,1664]{1,0:T(8,128)(2,1)S(1)} %collective-permute-done.4.refs_1_, bf16[64,1664]{1,0:T(8,128)(2,1)S(1)} %collective-permute-done.5.refs_2_, ...), custom_call_target="tpu_custom_call" | custom-call | tf_op jit(solution)/shard_map/gather/pallas_call | solution.py:240
  60.2 0.0 collective-permute-done.23.refs_3_
  60.2 0.0 collective-permute-done.18.refs_1_
  60.3 3.6 %convolve.3 = (f32[2,16,1536]{2,1,0:T(8,128)S(1)}, bf16[2,16,1536]{2,1,0:T(8,128)(2,1)S(1)}) custom-call(bf16[256,1664]{1,0:T(8,128)(2,1)S(1)} %gather.1.dense, bf16[4,8,32,128]{3,2,1,0:T(8,128)(2,1)S(1)} %get-tuple-element.20.refs_0_, bf16[4,8,32,128]{3,2,1,0:T(8,128)(2,1)S(1)} %collective-permute-done.18.refs_1_, ...), custom_call_target="tpu_custom_call" | custom-call | tf_op jit(solution)/shard_map/convolve/pallas_call | solution.py:326
  63.8 0.1 collective-permute-start.24
  63.9 0.0 collective-permute-done.20.refs_3_
  63.9 3.5 %convolve.2 = (f32[2,16,1536]{2,1,0:T(8,128)S(1)}, bf16[2,16,1536]{2,1,0:T(8,128)(2,1)S(1)}) custom-call(bf16[256,1664]{1,0:T(8,128)(2,1)S(1)} %gather.1.dense, bf16[4,8,32,128]{3,2,1,0:T(8,128)(2,1)S(1)} %get-tuple-element.20.refs_0_, bf16[4,8,32,128]{3,2,1,0:T(8,128)(2,1)S(1)} %collective-permute-done.18.refs_1_, ...), custom_call_target="tpu_custom_call" | custom-call | tf_op jit(solution)/shard_map/convolve/pallas_call | solution.py:326
  67.4 2.1 %collective-permute-start.21 = (bf16[2,16,1536]{2,1,0:T(8,128)(2,1)S(1)}, bf16[2,16,1536]{2,1,0:T(8,128)(2,1)S(1)}, u32[]{:S(2)}, u32[]{:S(2)}) collective-permute-start(bf16[2,16,1536]{2,1,0:T(8,128)(2,1)S(1)} %get-tuple-element.23), channel_id=1, source_target_pairs={{0,1},{1,0},{2,3},{3,2},{4,5},{5,4},{6,7},{7,6},{8,9},{9,8},{10,11... | collective-permute-start | bytes 294920 | tf_op jit(solution)/shard_map/ppermute | solution.py:382
  69.5 0.0 collective-permute-done.24.got_ref
  69.5 0.8 %assemble.2.refs_0_ = f32[4,3,16,1024]{3,2,1,0:T(8,128)} custom-call(f32[2,16,1536]{2,1,0:T(8,128)S(1)} %get-tuple-element.25.own_ref, bf16[2,16,1536]{2,1,0:T(8,128)(2,1)S(1)} %collective-permute-done.24.got_ref), custom_call_target="tpu_custom_call" | custom-call | tf_op jit(solution)/shard_map/assemble/pallas_call | solution.py:369
  70.3 1.9 %collective-permute-done.21.got_ref = bf16[2,16,1536]{2,1,0:T(8,128)(2,1)S(1)} collective-permute-done((bf16[2,16,1536]{2,1,0:T(8,128)(2,1)S(1)}, bf16[2,16,1536]{2,1,0:T(8,128)(2,1)S(1)}, u32[]{:S(2)}, u32[]{:S(2)}) %collective-permute-start.21) | collective-permute-done | bytes 98336 | tf_op jit(solution)/shard_map/ppermute | solution.py:382
  72.1 0.8 %assemble.3 = f32[4,3,16,1024]{3,2,1,0:T(8,128)} custom-call(f32[2,16,1536]{2,1,0:T(8,128)S(1)} %get-tuple-element.22.own_ref, bf16[2,16,1536]{2,1,0:T(8,128)(2,1)S(1)} %collective-permute-done.21.got_ref, f32[4,3,16,1024]{3,2,1,0:T(8,128)} %assemble.2.refs_0_), custom_call_target="tpu_custom_call", output_to_operand_aliasing={{}: (2, {})} | custom-call | tf_op jit(solution)/shard_map/assemble/pallas_call | solution.py:369
  (17 shorter events, 0.1 us)
Async XLA Ops:
  0.7 18.3 %collective-permute-start.3 = (s32[32]{0:T(128)S(1)}, s32[32]{0:T(128)S(1)}, u32[]{:S(2)}, u32[]{:S(2)}) collective-permute-start(s32[32]{0:T(128)S(1)} %bitcast_add_fusion), channel_id=1, source_target_pairs={{0,3},{1,2},{2,1},{3,0},{4,7},{5,6},{6,5},{7,4},{8,11},{9,10},{10,... | collective-permute-start | bytes 392 | tf_op jit(solution)/shard_map/ppermute | solution.py:382
  5.8 12.6 %collective-permute-start.2 = (s32[32]{0:T(128)S(1)}, s32[32]{0:T(128)S(1)}, u32[]{:S(2)}, u32[]{:S(2)}) collective-permute-start(s32[32]{0:T(128)S(1)} %bitcast_add_fusion), channel_id=1, source_target_pairs={{0,2},{1,3},{2,0},{3,1},{4,6},{5,7},{6,4},{7,5},{8,10},{9,11},{10,... | collective-permute-start | bytes 392 | tf_op jit(solution)/shard_map/ppermute | solution.py:382
  5.8 11.0 %collective-permute-start.1 = (s32[32]{0:T(128)S(1)}, s32[32]{0:T(128)S(1)}, u32[]{:S(2)}, u32[]{:S(2)}) collective-permute-start(s32[32]{0:T(128)S(1)} %bitcast_add_fusion), channel_id=1, source_target_pairs={{0,1},{1,0},{2,3},{3,2},{4,5},{5,4},{6,7},{7,6},{8,9},{9,8},{10,11... | collective-permute-start | bytes 392 | tf_op jit(solution)/shard_map/ppermute | solution.py:382
  6.3 1.7 %copy-start = (bf16[64,6,3,1024]{3,0,2,1:T(8,128)(2,1)S(1)}, bf16[64,6,3,1024]{3,0,2,1:T(8,128)(2,1)}, u32[]{:S(2)}) copy-start(bf16[64,6,3,1024]{3,0,2,1:T(8,128)(2,1)} %param.5) | copy-start | bytes 7077892
  8.0 0.7 copy-start.4
  8.7 5.1 %copy-start.1 = (bf16[32,64,128]{2,1,0:T(8,128)(2,1)S(1)}, bf16[32,64,128]{2,1,0:T(8,128)(2,1)}, u32[]{:S(2)}) copy-start(bf16[32,64,128]{2,1,0:T(8,128)(2,1)} %slip_ref.1) | copy-start | bytes 1572868
  9.8 24.5 %collective-permute-start.4 = (bf16[64,1664]{1,0:T(8,128)(2,1)S(1)}, bf16[64,1664]{1,0:T(8,128)(2,1)S(1)}, u32[]{:S(2)}, u32[]{:S(2)}) collective-permute-start(bf16[64,1664]{1,0:T(8,128)(2,1)S(1)} %get-tuple-element.16), channel_id=1, source_target_pairs={{0,1},{1,0},{2,3},{3,2},{4,5},{5,4},{6,7},{7,6},{8,9},{9,8},{10,11... | collective-permute-start | bytes 638984 | tf_op jit(solution)/shard_map/ppermute | solution.py:382
  11.3 25.3 %collective-permute-start = (bf16[64,1664]{1,0:T(8,128)(2,1)S(1)}, bf16[64,1664]{1,0:T(8,128)(2,1)S(1)}, u32[]{:S(2)}, u32[]{:S(2)}) collective-permute-start(bf16[64,1664]{1,0:T(8,128)(2,1)S(1)} %get-tuple-element.16), channel_id=1, source_target_pairs={{0,3},{1,2},{2,1},{3,0},{4,7},{5,6},{6,5},{7,4},{8,11},{9,10},{10,... | collective-permute-start | bytes 638984 | tf_op jit(solution)/shard_map/ppermute | solution.py:382
  16.7 19.8 %collective-permute-start.10 = (bf16[64,1664]{1,0:T(8,128)(2,1)S(1)}, bf16[64,1664]{1,0:T(8,128)(2,1)S(1)}, u32[]{:S(2)}, u32[]{:S(2)}) collective-permute-start(bf16[64,1664]{1,0:T(8,128)(2,1)S(1)} %get-tuple-element.18.refs_0_), channel_id=1, source_target_pairs={{0,8},{4,12},{8,0},{12,4},{1,9},{5,13},{9,1},{13,5},{2,10},{6,14},... | collective-permute-start | bytes 638984 | tf_op jit(solution)/shard_map/ppermute | solution.py:382
  18.4 13.1 %collective-permute-start.19 = (bf16[2,8,32,128]{3,2,1,0:T(8,128)(2,1)S(1)}, bf16[2,8,32,128]{3,2,1,0:T(8,128)(2,1)S(1)}, u32[]{:S(2)}, u32[]{:S(2)}) collective-permute-start(bf16[2,8,32,128]{3,2,1,0:T(8,128)(2,1)S(1)} %get-tuple-element.21), channel_id=1, source_target_pairs={{0,2},{1,3},{2,0},{3,1},{4,6},{5,7},{6,4},{7,5},{8,10},{9,11},{10,... | collective-permute-start | bytes 393224 | tf_op jit(solution)/shard_map/ppermute | solution.py:382
  19.0 15.2 %collective-permute-start.22 = (bf16[2,8,32,128]{3,2,1,0:T(8,128)(2,1)S(1)}, bf16[2,8,32,128]{3,2,1,0:T(8,128)(2,1)}, u32[]{:S(2)}, u32[]{:S(2)}) collective-permute-start(bf16[2,8,32,128]{3,2,1,0:T(8,128)(2,1)S(1)} %get-tuple-element.24), channel_id=1, source_target_pairs={{0,2},{1,3},{2,0},{3,1},{4,6},{5,7},{6,4},{7,5},{8,10},{9,11},{10,... | collective-permute-start | bytes 393224 | tf_op jit(solution)/shard_map/ppermute | solution.py:382
  31.5 5.7 %collective-permute-start.6 = (bf16[64,1664]{1,0:T(8,128)(2,1)S(1)}, bf16[64,1664]{1,0:T(8,128)(2,1)S(1)}, u32[]{:S(2)}, u32[]{:S(2)}) collective-permute-start(bf16[64,1664]{1,0:T(8,128)(2,1)S(1)} %get-tuple-element.18.refs_0_), channel_id=1, source_target_pairs={{0,4},{4,0},{8,12},{12,8},{1,5},{5,1},{9,13},{13,9},{2,6},{6,2},{1... | collective-permute-start | bytes 638984 | tf_op jit(solution)/shard_map/ppermute | solution.py:382
  34.2 11.6 %collective-permute-start.5 = (bf16[64,1664]{1,0:T(8,128)(2,1)S(1)}, bf16[64,1664]{1,0:T(8,128)(2,1)S(1)}, u32[]{:S(2)}, u32[]{:S(2)}) collective-permute-start(bf16[64,1664]{1,0:T(8,128)(2,1)S(1)} %get-tuple-element.18.refs_0_), channel_id=1, source_target_pairs={{0,2},{1,3},{2,0},{3,1},{4,6},{5,7},{6,4},{7,5},{8,10},{9,11},{10,... | collective-permute-start | bytes 638984 | tf_op jit(solution)/shard_map/ppermute | solution.py:382
  34.3 11.6 %collective-permute-start.11 = (bf16[64,1664]{1,0:T(8,128)(2,1)S(1)}, bf16[64,1664]{1,0:T(8,128)(2,1)S(1)}, u32[]{:S(2)}, u32[]{:S(2)}) collective-permute-start(bf16[64,1664]{1,0:T(8,128)(2,1)S(1)} %collective-permute-done.4.refs_1_), channel_id=1, source_target_pairs={{0,8},{4,12},{8,0},{12,4},{1,9},{5,13},{9,1},{13,5},{2,10},{6,14},... | collective-permute-start | bytes 638984 | tf_op jit(solution)/shard_map/ppermute | solution.py:382
  36.6 10.8 %collective-permute-start.7 = (bf16[64,1664]{1,0:T(8,128)(2,1)S(1)}, bf16[64,1664]{1,0:T(8,128)(2,1)S(1)}, u32[]{:S(2)}, u32[]{:S(2)}) collective-permute-start(bf16[64,1664]{1,0:T(8,128)(2,1)S(1)} %collective-permute-done.4.refs_1_), channel_id=1, source_target_pairs={{0,4},{4,0},{8,12},{12,8},{1,5},{5,1},{9,13},{13,9},{2,6},{6,2},{1... | collective-permute-start | bytes 638984 | tf_op jit(solution)/shard_map/ppermute | solution.py:382
  36.6 11.0 %collective-permute-start.13 = (bf16[64,1664]{1,0:T(8,128)(2,1)S(1)}, bf16[64,1664]{1,0:T(8,128)(2,1)S(1)}, u32[]{:S(2)}, u32[]{:S(2)}) collective-permute-start(bf16[64,1664]{1,0:T(8,128)(2,1)S(1)} %collective-permute-done.refs_3_), channel_id=1, source_target_pairs={{0,8},{4,12},{8,0},{12,4},{1,9},{5,13},{9,1},{13,5},{2,10},{6,14},... | collective-permute-start | bytes 638984 | tf_op jit(solution)/shard_map/ppermute | solution.py:382
  37.2 10.7 %collective-permute-start.9 = (bf16[64,1664]{1,0:T(8,128)(2,1)S(1)}, bf16[64,1664]{1,0:T(8,128)(2,1)S(1)}, u32[]{:S(2)}, u32[]{:S(2)}) collective-permute-start(bf16[64,1664]{1,0:T(8,128)(2,1)S(1)} %collective-permute-done.refs_3_), channel_id=1, source_target_pairs={{0,4},{4,0},{8,12},{12,8},{1,5},{5,1},{9,13},{13,9},{2,6},{6,2},{1... | collective-permute-start | bytes 638984 | tf_op jit(solution)/shard_map/ppermute | solution.py:382
  45.8 2.1 %collective-permute-start.14 = (bf16[64,1664]{1,0:T(8,128)(2,1)S(1)}, bf16[64,1664]{1,0:T(8,128)(2,1)S(1)}, u32[]{:S(2)}, u32[]{:S(2)}) collective-permute-start(bf16[64,1664]{1,0:T(8,128)(2,1)S(1)} %collective-permute-done.10.refs_8_), channel_id=1, source_target_pairs={{0,4},{4,0},{8,12},{12,8},{1,5},{5,1},{9,13},{13,9},{2,6},{6,2},{1... | collective-permute-start | bytes 638984 | tf_op jit(solution)/shard_map/ppermute | solution.py:382
  45.9 7.7 %collective-permute-start.12 = (bf16[64,1664]{1,0:T(8,128)(2,1)S(1)}, bf16[64,1664]{1,0:T(8,128)(2,1)S(1)}, u32[]{:S(2)}, u32[]{:S(2)}) collective-permute-start(bf16[64,1664]{1,0:T(8,128)(2,1)S(1)} %collective-permute-done.5.refs_2_), channel_id=1, source_target_pairs={{0,8},{4,12},{8,0},{12,4},{1,9},{5,13},{9,1},{13,5},{2,10},{6,14},... | collective-permute-start | bytes 638984 | tf_op jit(solution)/shard_map/ppermute | solution.py:382
  47.4 6.1 %collective-permute-start.8 = (bf16[64,1664]{1,0:T(8,128)(2,1)S(1)}, bf16[64,1664]{1,0:T(8,128)(2,1)S(1)}, u32[]{:S(2)}, u32[]{:S(2)}) collective-permute-start(bf16[64,1664]{1,0:T(8,128)(2,1)S(1)} %collective-permute-done.5.refs_2_), channel_id=1, source_target_pairs={{0,4},{4,0},{8,12},{12,8},{1,5},{5,1},{9,13},{13,9},{2,6},{6,2},{1... | collective-permute-start | bytes 638984 | tf_op jit(solution)/shard_map/ppermute | solution.py:382
  47.6 5.9 %collective-permute-start.15 = (bf16[64,1664]{1,0:T(8,128)(2,1)S(1)}, bf16[64,1664]{1,0:T(8,128)(2,1)S(1)}, u32[]{:S(2)}, u32[]{:S(2)}) collective-permute-start(bf16[64,1664]{1,0:T(8,128)(2,1)S(1)} %collective-permute-done.11.refs_9_), channel_id=1, source_target_pairs={{0,4},{4,0},{8,12},{12,8},{1,5},{5,1},{9,13},{13,9},{2,6},{6,2},{1... | collective-permute-start | bytes 638984 | tf_op jit(solution)/shard_map/ppermute | solution.py:382
  47.9 12.3 %collective-permute-start.18 = (bf16[4,8,32,128]{3,2,1,0:T(8,128)(2,1)S(1)}, bf16[4,8,32,128]{3,2,1,0:T(8,128)(2,1)S(1)}, u32[]{:S(2)}, u32[]{:S(2)}) collective-permute-start(bf16[4,8,32,128]{3,2,1,0:T(8,128)(2,1)S(1)} %get-tuple-element.20.refs_0_), channel_id=1, source_target_pairs={{0,1},{1,0},{2,3},{3,2},{4,5},{5,4},{6,7},{7,6},{8,9},{9,8},{10,11... | collective-permute-start | bytes 786440 | tf_op jit(solution)/shard_map/ppermute | solution.py:382
  47.9 9.1 %collective-permute-start.17 = (bf16[64,1664]{1,0:T(8,128)(2,1)S(1)}, bf16[64,1664]{1,0:T(8,128)(2,1)}, u32[]{:S(2)}, u32[]{:S(2)}) collective-permute-start(bf16[64,1664]{1,0:T(8,128)(2,1)S(1)} %collective-permute-done.13.refs_11_), channel_id=1, source_target_pairs={{0,4},{4,0},{8,12},{12,8},{1,5},{5,1},{9,13},{13,9},{2,6},{6,2},{1... | collective-permute-start | bytes 638984 | tf_op jit(solution)/shard_map/ppermute | solution.py:382
  53.5 3.5 %collective-permute-start.16 = (bf16[64,1664]{1,0:T(8,128)(2,1)S(1)}, bf16[64,1664]{1,0:T(8,128)(2,1)}, u32[]{:S(2)}, u32[]{:S(2)}) collective-permute-start(bf16[64,1664]{1,0:T(8,128)(2,1)S(1)} %collective-permute-done.12.refs_10_), channel_id=1, source_target_pairs={{0,4},{4,0},{8,12},{12,8},{1,5},{5,1},{9,13},{13,9},{2,6},{6,2},{1... | collective-permute-start | bytes 638984 | tf_op jit(solution)/shard_map/ppermute | solution.py:382
  53.5 6.7 %collective-permute-start.23 = (bf16[2,8,32,128]{3,2,1,0:T(8,128)(2,1)}, bf16[2,8,32,128]{3,2,1,0:T(8,128)(2,1)}, u32[]{:S(2)}, u32[]{:S(2)}) collective-permute-start(bf16[2,8,32,128]{3,2,1,0:T(8,128)(2,1)} %collective-permute-done.22.refs_2_), channel_id=1, source_target_pairs={{0,1},{1,0},{2,3},{3,2},{4,5},{5,4},{6,7},{7,6},{8,9},{9,8},{10,11... | collective-permute-start | bytes 393224 | tf_op jit(solution)/shard_map/ppermute | solution.py:382
  53.5 0.7 copy-start.2
  54.2 9.7 %collective-permute-start.20 = (bf16[2,8,32,128]{3,2,1,0:T(8,128)(2,1)S(1)}, bf16[2,8,32,128]{3,2,1,0:T(8,128)(2,1)}, u32[]{:S(2)}, u32[]{:S(2)}) collective-permute-start(bf16[2,8,32,128]{3,2,1,0:T(8,128)(2,1)S(1)} %collective-permute-done.19.refs_2_), channel_id=1, source_target_pairs={{0,1},{1,0},{2,3},{3,2},{4,5},{5,4},{6,7},{7,6},{8,9},{9,8},{10,11... | collective-permute-start | bytes 393224 | tf_op jit(solution)/shard_map/ppermute | solution.py:382
  57.0 0.9 %copy-start.3 = (bf16[64,1664]{1,0:T(8,128)(2,1)S(1)}, bf16[64,1664]{1,0:T(8,128)(2,1)}, u32[]{:S(2)}) copy-start(bf16[64,1664]{1,0:T(8,128)(2,1)} %copy-done.2) | copy-start | bytes 638980
  63.8 5.7 %collective-permute-start.24 = (bf16[2,16,1536]{2,1,0:T(8,128)(2,1)S(1)}, bf16[2,16,1536]{2,1,0:T(8,128)(2,1)S(1)}, u32[]{:S(2)}, u32[]{:S(2)}) collective-permute-start(bf16[2,16,1536]{2,1,0:T(8,128)(2,1)S(1)} %get-tuple-element.26), channel_id=1, source_target_pairs={{0,1},{1,0},{2,3},{3,2},{4,5},{5,4},{6,7},{7,6},{8,9},{9,8},{10,11... | collective-permute-start | bytes 294920 | tf_op jit(solution)/shard_map/ppermute | solution.py:382
  67.4 4.7 %collective-permute-start.21 = (bf16[2,16,1536]{2,1,0:T(8,128)(2,1)S(1)}, bf16[2,16,1536]{2,1,0:T(8,128)(2,1)S(1)}, u32[]{:S(2)}, u32[]{:S(2)}) collective-permute-start(bf16[2,16,1536]{2,1,0:T(8,128)(2,1)S(1)} %get-tuple-element.23), channel_id=1, source_target_pairs={{0,1},{1,0},{2,3},{3,2},{4,5},{5,4},{6,7},{7,6},{8,9},{9,8},{10,11... | collective-permute-start | bytes 294920 | tf_op jit(solution)/shard_map/ppermute | solution.py:382
where the time goes:
time: 73.2 us; the launch traced here: 72.9 us
  waiting for transfers between devices  28.3 us (39%)
  starting transfers between devices  23 us (31%)
  Pallas kernels  14.8 us (20%)
  local copies, waits for them, and re-layouts  5.84 us (8%)
  other arithmetic  0.8 us (1%)
    ppermute x25, waiting for transfers between devices, swap(): lax.ppermute(value, axis, [(i, i ^ flip) for i in range(lax.axis_size(axi...  28.3 us
    ppermute x25, starting transfers between devices, swap(): lax.ppermute(value, axis, [(i, i ^ flip) for i in range(lax.axis_size(axi...  23 us
    pallas_call x2, Pallas kernels, convolve(): pl.pallas_call(functools.partial(convolve_kernel, base), in_specs=[vmem]...  7.06 us
    unnamed x13, local copies, waits for them, and re-layouts  3.98 us
    pallas_call x1, Pallas kernels, turn_slip(): pl.pallas_call(turn_kernel, in_specs=[vmem], out_specs=[vmem] * len(outs)...  2.9 us
    pallas_call x1, Pallas kernels, gather(): pl.pallas_call(gather_kernel, in_specs=[vmem] * (1 + len(green)), out_spe...  2.25 us
    pallas_call x2, Pallas kernels, assemble(): pl.pallas_call(assemble_kernel, grid=(slots,), in_specs=[spec, spec] + [p...  1.52 us
  transfers between devices with their start and end apart: 25, of which 5 were waited for; matrix products, arithmetic and copies ran while one was open for 3% of the time, Pallas kernels for 19%

commit v1 on v0

--- a/solution.py
+++ b/solution.py
@@ -86,56 +86,65 @@
     return lax.psum_scatter(partial_value, "worker", scatter_dimension=1, tiled=True)
 
 
-def combine_kernel(samples, sgt_ref, mech_ref, same_ref, other_ref, mech_scratch):
-    step = pl.program_id(0)
-    count = same_ref.shape[0]
-
-    @pl.when(step == 0)
-    def _():
-        mech_scratch[...] = jnp.transpose(mech_ref[...].astype(F32))
-
-    mech = mech_scratch[pl.ds(pl.multiple_of(step * count, count), count), :]
-    green = []
-    for k in range(3):
-        total = mech[:, 0:1] * sgt_ref[0, k].astype(F32)
-        for comp in range(1, 6):
-            total = total + mech[:, comp : comp + 1] * sgt_ref[comp, k].astype(F32)
-        green.append(total.astype(BF))
+def combine_kernel(samples, sgt_ref, mech_ref, same_ref, other_ref, mech_scratch, sgt_scratch, sems):
+    steps, comps, _, count, _ = sgt_scratch.shape
+
+    def copy(step):
+        rows = pl.ds(pl.multiple_of(step * count, count), count)
+        return pltpu.make_async_copy(sgt_ref.at[:, :, rows, :], sgt_scratch.at[step], sems.at[step])
+
+    for step in range(steps):
+        copy(step).start()
+    mech_scratch[...] = jnp.transpose(mech_ref[...].astype(F32))
     half = samples // 2
     parity = lax.rem(lax.axis_index("worker"), 2)
 
-    def write(low_ref, high_ref):
-        low_ref[:, :samples] = green[0]
-        low_ref[:, samples : samples + LANES] = jnp.zeros((count, LANES), BF)
-        low_ref[:, samples + LANES :] = green[1][:, :half]
-        high_ref[:, :samples] = green[2]
-        high_ref[:, samples:] = green[1][:, half - LANES :]
-
-    @pl.when(parity == 0)
-    def _():
-        write(same_ref, other_ref)
-
-    @pl.when(parity == 1)
-    def _():
-        write(other_ref, same_ref)
+    @pl.loop(0, steps)
+    def _(step):
+        copy(step).wait()
+        rows = pl.ds(pl.multiple_of(step * count, count), count)
+        mech = mech_scratch[rows, :]
+        green = []
+        for k in range(3):
+            total = mech[:, 0:1] * sgt_scratch[step, 0, k].astype(F32)
+            for comp in range(1, comps):
+                total = total + mech[:, comp : comp + 1] * sgt_scratch[step, comp, k].astype(F32)
+            green.append(total.astype(BF))
+
+        def write(low_ref, high_ref):
+            low_ref[rows, :samples] = green[0]
+            low_ref[rows, samples : samples + LANES] = jnp.zeros((count, LANES), BF)
+            low_ref[rows, samples + LANES :] = green[1][:, :half]
+            high_ref[rows, :samples] = green[2]
+            high_ref[rows, samples:] = green[1][:, half - LANES :]
+
+        @pl.when(parity == 0)
+        def _():
+            write(same_ref, other_ref)
+
+        @pl.when(parity == 1)
+        def _():
+            write(other_ref, same_ref)
 
 
 def combine(sgt, mechanism):
     points, comps, kinds, samples = sgt.shape
     width = samples + LANES + samples // 2
-    step = min(16, points)
+    count = min(16, points)
+    steps = points // count
     out = jax.ShapeDtypeStruct((points, width), BF)
+    vmem = pl.BlockSpec(memory_space=pltpu.VMEM)
     return pl.pallas_call(
         functools.partial(combine_kernel, samples),
-        grid=(points // step,),
-        in_specs=[
-            pl.BlockSpec((comps, kinds, step, samples), lambda p: (0, 0, p, 0)),
-            pl.BlockSpec((comps, points), lambda p: (0, 0)),
+        in_specs=[pl.BlockSpec(memory_space=pltpu.HBM), vmem],
+        out_specs=[vmem] * 2,
+        out_shape=[out, out],
+        scratch_shapes=[
+            pltpu.VMEM((points, comps), F32),
+            pltpu.VMEM((steps, comps, kinds, count, samples), BF),
+            pltpu.SemaphoreType.DMA((steps,)),
         ],
-        out_specs=[pl.BlockSpec((step, width), lambda p: (p, 0))] * 2,
-        out_shape=[out, out],
-        scratch_shapes=[pltpu.VMEM((points, comps), F32)],
-        compiler_params=pltpu.CompilerParams(vmem_limit_bytes=16 * MIB),
+        compiler_params=pltpu.CompilerParams(vmem_limit_bytes=8 * MIB),
         name="combine",
     )(jnp.transpose(sgt, (1, 2, 0, 3)), mechanism)
 
@@ -212,15 +221,30 @@
     )(slip)
 
 
-def gather_kernel(rows_ref, *refs):
-    green, dense, hot = refs[:-2], refs[-2], refs[-1]
+def gather_kernel(sources, *refs):
+    codes, green, dense, hot = refs[:sources], refs[sources:-2], refs[-2], refs[-1]
     pieces = len(green)
     points, width = green[0].shape
+    blocks_here = points // BLK
+    requests = codes[0].shape[0] // RUP_SLOTS
+    handler, worker = lax.axis_index("handler"), lax.axis_index("worker")
+    tall = requests * BLK
     span = 2 * LANES
-    asked = rows_ref[...]
-    for c in range(0, pieces * points, LANES):
-        column = lax.broadcasted_iota(jnp.int32, (asked.shape[0], LANES), 1) + c
-        hot[:, c : c + LANES] = jnp.where(asked == column, 1.0, 0.0).astype(BF)
+    row = lax.broadcasted_iota(jnp.int32, (tall, LANES), 0)
+    lane = lax.broadcasted_iota(jnp.int32, (tall, LANES), 1)
+    for slot in range(RUP_SLOTS):
+        for j in range(sources):
+            asked = jnp.zeros((tall, LANES), jnp.int32)
+            for n in range(requests):
+                code = codes[j][slot * requests + n]
+                owner = code // blocks_here
+                piece = ((owner // sources) ^ handler) * sources + (lax.rem(owner, sources) ^ worker)
+                base = piece * points + lax.rem(code, blocks_here) * BLK - n * BLK
+                asked = jnp.where(row >= n * BLK, base, asked)
+            asked = asked + row - lane
+            put = (slot * sources + j) * tall
+            for c in range(0, pieces * points, LANES):
+                hot[put : put + tall, c : c + LANES] = jnp.where(asked == c, 1.0, 0.0).astype(BF)
     together = max(1, span // points)
     for c in range(0, width, span):
         e = min(width, c + span)
@@ -234,18 +258,19 @@
         dense[:, c:e] = total.astype(BF)
 
 
-def gather(rows, green):
+def gather(codes, green):
     points, width = green[0].shape
+    asked = len(codes) * codes[0].shape[0] * BLK
     vmem = pl.BlockSpec(memory_space=pltpu.VMEM)
     return pl.pallas_call(
-        gather_kernel,
-        in_specs=[vmem] * (1 + len(green)),
+        functools.partial(gather_kernel, len(codes)),
+        in_specs=[pl.BlockSpec(memory_space=pltpu.SMEM)] * len(codes) + [vmem] * len(green),
         out_specs=vmem,
-        out_shape=jax.ShapeDtypeStruct((rows.shape[0], width), BF),
-        scratch_shapes=[pltpu.VMEM((rows.shape[0], len(green) * points), BF)],
+        out_shape=jax.ShapeDtypeStruct((asked, width), BF),
+        scratch_shapes=[pltpu.VMEM((asked, len(green) * points), BF)],
         compiler_params=pltpu.CompilerParams(vmem_limit_bytes=8 * MIB),
         name="gather",
-    )(rows, *green)
+    )(*codes, *green)
 
 
 def convolve_kernel(base, dense, *refs):
@@ -384,30 +409,21 @@
 
 def local_replicate(sgt, mechanism, req_owner, req_local, slip):
     handlers, workers = lax.axis_size("handler"), lax.axis_size("worker")
-    handler, worker = lax.axis_index("handler"), lax.axis_index("worker")
     points, _, _, samples = sgt.shape
-    blocks_here = points // BLK
-    requests = req_local.shape[0]
     same, other = combine(sgt, mechanism)
 
-    code = req_owner[:, 0] * blocks_here + req_local
-    codes = jnp.stack([code] + [swap(code, "worker", flip) for flip in range(1, workers)])
-    owner = codes // blocks_here
-    piece = ((owner // workers) ^ handler) * workers + ((owner % workers) ^ worker)
-    row = piece * points + codes % blocks_here * BLK
-    row = jnp.transpose(row.reshape(workers, RUP_SLOTS, requests // RUP_SLOTS), (1, 0, 2))
-    rows = (row[..., None] + jnp.arange(BLK, dtype=jnp.int32)).reshape(-1, 1)
+    code = req_owner[:, 0] * (points // BLK) + req_local
+    codes = [code] + [swap(code, "worker", flip) for flip in range(1, workers)]
 
     green = {(0, 0): same}
     for flip in range(1, workers):
         green[0, flip] = swap(other if flip % 2 else same, "worker", flip)
-    green[0, workers - 1], rows = lax.optimization_barrier((green[0, workers - 1], rows))
     bit = handlers // 2
     while bit:
         for (hand, flip), value in list(green.items()):
             green[hand ^ bit, flip] = swap(value, "handler", bit)
         bit //= 2
-    dense = gather(rows, [green[hand, flip] for hand in range(handlers) for flip in range(workers)])
+    dense = gather(codes, [green[hand, flip] for hand in range(handlers) for flip in range(workers)])
 
     turned = turn_slip(slip, workers)
     near = [turned[0], swap(turned[0], "worker", 1)]

time: 73.2 us -> 72.8 us (level)
  starting transfers between devices: 23 us -> 30.9 us
  local copies, waits for them, and re-layouts: 5.84 us -> 2.38 us
  waiting for transfers between devices: 28.3 us -> 25.7 us
  Pallas kernels: 14.8 us -> 13.5 us
  other arithmetic: 0.8 us -> 0.01 us
    ppermute x25, starting transfers between devices: 23 us -> 30.9 us  [swap(): lax.ppermute(value, axis, [(i, i ^ flip) for i in range(lax.axis_size(axi...]
    ppermute x25, waiting for transfers between devices: 28.3 us -> 25.7 us  [swap(): lax.ppermute(value, axis, [(i, i ^ flip) for i in range(lax.axis_size(axi...]
    pallas_call x2, Pallas kernels: 7.06 us -> 5.19 us  [convolve(): pl.pallas_call(functools.partial(convolve_kernel, base), in_specs=[vmem]...]
    unnamed x13 -> x10, local copies, waits for them, and re-layouts: 3.98 us -> 2.38 us
    optimization_barrier x1 -> x0, local copies, waits for them, and re-layouts: 0.79 us -> none  [local_replicate(): lax.optimization_barrier((green[0, workers - 1], rows))]
    add x2 -> x1, other arithmetic: 0.75 us -> 0.01 us  [local_replicate(): code = req_owner[:, 0] * (points // BLK) + req_local]
  transfers between devices with their start and end apart: 25 -> 25, of which waited for: 5 -> 9; matrix products, arithmetic and copies ran while one was open for 3% -> 0% of each run, Pallas kernels for 19% -> 16%
where the time goes in v1:
time: 72.8 us; the launch traced here: 72.6 us
  starting transfers between devices  30.9 us (42%)
  waiting for transfers between devices  25.7 us (35%)
  Pallas kernels  13.5 us (19%)
  local copies, waits for them, and re-layouts  2.38 us (3%)
    ppermute x25, starting transfers between devices, swap(): lax.ppermute(value, axis, [(i, i ^ flip) for i in range(lax.axis_size(axi...  30.9 us
    ppermute x25, waiting for transfers between devices, swap(): lax.ppermute(value, axis, [(i, i ^ flip) for i in range(lax.axis_size(axi...  25.7 us
    pallas_call x2, Pallas kernels, convolve(): pl.pallas_call(functools.partial(convolve_kernel, base), in_specs=[vmem]...  5.19 us
    pallas_call x1, Pallas kernels, gather(): pl.pallas_call(functools.partial(gather_kernel, len(codes)), in_specs=[pl...  2.98 us
    pallas_call x1, Pallas kernels, turn_slip(): pl.pallas_call(turn_kernel, in_specs=[vmem], out_specs=[vmem] * len(outs)...  2.9 us
    unnamed x10, local copies, waits for them, and re-layouts  2.38 us
    pallas_call x2, Pallas kernels, assemble(): pl.pallas_call(assemble_kernel, grid=(slots,), in_specs=[spec, spec] + [p...  1.52 us
  transfers between devices with their start and end apart: 25, of which 9 were waited for; matrix products, arithmetic and copies ran while one was open for 0% of the time, Pallas kernels for 16%

profile of v1, /device:TPU:0, one launch (start us, length us, event | category | flops | bytes accessed | tf_op | source)
XLA Modules:
  0.0 72.6 jit_solution(17653916036261908913)
XLA Ops:
  0.0 0.0 copy-start.3
  0.0 0.0 copy-start.4
  0.0 1.7 %copy-done = bf16[64,6,3,1024]{3,0,2,1:T(8,128)(2,1)S(1)} copy-done((bf16[64,6,3,1024]{3,0,2,1:T(8,128)(2,1)S(1)}, bf16[64,6,3,1024]{3,0,2,1:T(8,128)(2,1)}, u32[]{:S(2)}) %copy-start) | copy-done | bytes 2359320
  1.7 0.7 copy-done.2
  2.4 0.9 %combine.1 = (bf16[64,1664]{1,0:T(8,128)(2,1)S(1)}, bf16[64,1664]{1,0:T(8,128)(2,1)S(1)}) custom-call(bf16[6,3,64,1024]{3,2,1,0:T(8,128)(2,1)S(1)} %bitcast.4, bf16[6,64]{1,0:T(8,128)(2,1)S(1)} %copy-done.2), custom_call_target="tpu_custom_call" | custom-call | tf_op jit(solution)/shard_map/combine/pallas_call | solution.py:137
  3.3 5.1 %collective-permute-start.5 = (bf16[64,1664]{1,0:T(8,128)(2,1)S(1)}, bf16[64,1664]{1,0:T(8,128)(2,1)S(1)}, u32[]{:S(2)}, u32[]{:S(2)}) collective-permute-start(bf16[64,1664]{1,0:T(8,128)(2,1)S(1)} %get-tuple-element.15), channel_id=1, source_target_pairs={{0,3},{1,2},{2,1},{3,0},{4,7},{5,6},{6,5},{7,4},{8,11},{9,10},{10,... | collective-permute-start | bytes 638984 | tf_op jit(solution)/shard_map/ppermute | solution.py:407
  8.5 0.0 copy-done.1
  8.5 2.9 %turn_slip.1 = (bf16[4,8,32,128]{3,2,1,0:T(8,128)(2,1)S(1)}, bf16[2,8,32,128]{3,2,1,0:T(8,128)(2,1)S(1)}, bf16[2,8,32,128]{3,2,1,0:T(8,128)(2,1)S(1)}) custom-call(bf16[32,64,128]{2,1,0:T(8,128)(2,1)S(1)} %copy-done.1), custom_call_target="tpu_custom_call" | custom-call | tf_op jit(solution)/shard_map/turn_slip/pallas_call | solution.py:213
  11.4 0.1 collective-permute-start.19
  11.5 0.0 copy-done.3
  11.5 0.0 copy-done.4
  11.5 2.0 %collective-permute-start.2 = (s32[32]{0:T(128)S(1)}, s32[32]{0:T(128)S(1)}, u32[]{:S(2)}, u32[]{:S(2)}) collective-permute-start(s32[32]{0:T(128)S(1)} %bitcast_add_fusion.refs_0_), channel_id=1, source_target_pairs={{0,3},{1,2},{2,1},{3,0},{4,7},{5,6},{6,5},{7,4},{8,11},{9,10},{10,... | collective-permute-start | bytes 392 | tf_op jit(solution)/shard_map/ppermute | solution.py:407
  13.4 1.1 %collective-permute-start.22 = (bf16[2,8,32,128]{3,2,1,0:T(8,128)(2,1)S(1)}, bf16[2,8,32,128]{3,2,1,0:T(8,128)(2,1)S(1)}, u32[]{:S(2)}, u32[]{:S(2)}) collective-permute-start(bf16[2,8,32,128]{3,2,1,0:T(8,128)(2,1)S(1)} %get-tuple-element.20), channel_id=1, source_target_pairs={{0,2},{1,3},{2,0},{3,1},{4,6},{5,7},{6,4},{7,5},{8,10},{9,11},{10,... | collective-permute-start | bytes 393224 | tf_op jit(solution)/shard_map/ppermute | solution.py:407
  14.5 1.8 %collective-permute-start.1 = (s32[32]{0:T(128)S(1)}, s32[32]{0:T(128)S(1)}, u32[]{:S(2)}, u32[]{:S(2)}) collective-permute-start(s32[32]{0:T(128)S(1)} %bitcast_add_fusion.refs_0_), channel_id=1, source_target_pairs={{0,2},{1,3},{2,0},{3,1},{4,6},{5,7},{6,4},{7,5},{8,10},{9,11},{10,... | collective-permute-start | bytes 392 | tf_op jit(solution)/shard_map/ppermute | solution.py:407
  16.4 0.6 collective-permute-done.2.refs_3_
  17.0 10.4 %collective-permute-start.3 = (bf16[64,1664]{1,0:T(8,128)(2,1)S(1)}, bf16[64,1664]{1,0:T(8,128)(2,1)S(1)}, u32[]{:S(2)}, u32[]{:S(2)}) collective-permute-start(bf16[64,1664]{1,0:T(8,128)(2,1)S(1)} %get-tuple-element.15), channel_id=1, source_target_pairs={{0,1},{1,0},{2,3},{3,2},{4,5},{5,4},{6,7},{7,6},{8,9},{9,8},{10,11... | collective-permute-start | bytes 638984 | tf_op jit(solution)/shard_map/ppermute | solution.py:407
  27.4 1.5 %collective-permute-done.1.refs_2_ = s32[32]{0:T(128)S(1)} collective-permute-done((s32[32]{0:T(128)S(1)}, s32[32]{0:T(128)S(1)}, u32[]{:S(2)}, u32[]{:S(2)}) %collective-permute-start.1) | collective-permute-done | bytes 160 | tf_op jit(solution)/shard_map/ppermute | solution.py:407
  28.9 0.0 collective-permute-start
  28.9 4.5 %collective-permute-done.refs_1_ = s32[32]{0:T(128)S(1)} collective-permute-done((s32[32]{0:T(128)S(1)}, s32[32]{0:T(128)S(1)}, u32[]{:S(2)}, u32[]{:S(2)}) %collective-permute-start) | collective-permute-done | bytes 160 | tf_op jit(solution)/shard_map/ppermute | solution.py:407
  33.4 1.5 %collective-permute-start.10 = (bf16[64,1664]{1,0:T(8,128)(2,1)S(1)}, bf16[64,1664]{1,0:T(8,128)(2,1)S(1)}, u32[]{:S(2)}, u32[]{:S(2)}) collective-permute-start(bf16[64,1664]{1,0:T(8,128)(2,1)S(1)} %get-tuple-element.14.refs_4_), channel_id=1, source_target_pairs={{0,8},{4,12},{8,0},{12,4},{1,9},{5,13},{9,1},{13,5},{2,10},{6,14},... | collective-permute-start | bytes 638984 | tf_op jit(solution)/shard_map/ppermute | solution.py:407
  34.9 0.0 collective-permute-done.19.refs_2_
  34.9 0.0 collective-permute-start.6
  34.9 0.0 collective-permute-done.22.refs_2_
  34.9 1.2 %collective-permute-start.4 = (bf16[64,1664]{1,0:T(8,128)(2,1)S(1)}, bf16[64,1664]{1,0:T(8,128)(2,1)S(1)}, u32[]{:S(2)}, u32[]{:S(2)}) collective-permute-start(bf16[64,1664]{1,0:T(8,128)(2,1)S(1)} %get-tuple-element.14.refs_4_), channel_id=1, source_target_pairs={{0,2},{1,3},{2,0},{3,1},{4,6},{5,7},{6,4},{7,5},{8,10},{9,11},{10,... | collective-permute-start | bytes 638984 | tf_op jit(solution)/shard_map/ppermute | solution.py:407
  36.1 0.0 collective-permute-done.5.refs_7_
  36.1 0.5 collective-permute-start.13
  36.7 0.0 collective-permute-done.3.refs_5_
  36.7 0.0 collective-permute-start.9
  36.7 4.8 %collective-permute-done.10.refs_12_ = bf16[64,1664]{1,0:T(8,128)(2,1)S(1)} collective-permute-done((bf16[64,1664]{1,0:T(8,128)(2,1)S(1)}, bf16[64,1664]{1,0:T(8,128)(2,1)S(1)}, u32[]{:S(2)}, u32[]{:S(2)}) %collective-permute-start.10) | collective-permute-done | bytes 213024 | tf_op jit(solution)/shard_map/ppermute | solution.py:407
  41.5 1.5 %collective-permute-start.11 = (bf16[64,1664]{1,0:T(8,128)(2,1)S(1)}, bf16[64,1664]{1,0:T(8,128)(2,1)S(1)}, u32[]{:S(2)}, u32[]{:S(2)}) collective-permute-start(bf16[64,1664]{1,0:T(8,128)(2,1)S(1)} %collective-permute-done.3.refs_5_), channel_id=1, source_target_pairs={{0,8},{4,12},{8,0},{12,4},{1,9},{5,13},{9,1},{13,5},{2,10},{6,14},... | collective-permute-start | bytes 638984 | tf_op jit(solution)/shard_map/ppermute | solution.py:407
  43.0 0.0 collective-permute-done.6.refs_8_
  43.0 0.0 collective-permute-start.7
  43.0 4.8 %collective-permute-done.4.refs_6_ = bf16[64,1664]{1,0:T(8,128)(2,1)S(1)} collective-permute-done((bf16[64,1664]{1,0:T(8,128)(2,1)S(1)}, bf16[64,1664]{1,0:T(8,128)(2,1)S(1)}, u32[]{:S(2)}, u32[]{:S(2)}) %collective-permute-start.4) | collective-permute-done | bytes 213024 | tf_op jit(solution)/shard_map/ppermute | solution.py:407
  47.8 0.1 collective-permute-start.14
  47.9 0.0 collective-permute-done.13.refs_15_
  47.9 0.5 collective-permute-start.12
  48.5 0.0 collective-permute-done.9.refs_11_
  48.5 0.2 collective-permute-start.8
  48.6 0.8 %collective-permute-done.11.refs_13_ = bf16[64,1664]{1,0:T(8,128)(2,1)S(1)} collective-permute-done((bf16[64,1664]{1,0:T(8,128)(2,1)S(1)}, bf16[64,1664]{1,0:T(8,128)(2,1)S(1)}, u32[]{:S(2)}, u32[]{:S(2)}) %collective-permute-start.11) | collective-permute-done | bytes 213024 | tf_op jit(solution)/shard_map/ppermute | solution.py:407
  49.5 0.0 collective-permute-start.17
  49.5 0.0 collective-permute-done.7.refs_9_
  49.5 0.4 collective-permute-start.18
  49.9 0.0 collective-permute-done.14.refs_16_
  49.9 0.2 collective-permute-start.15
  50.1 5.4 %collective-permute-done.12.refs_14_ = bf16[64,1664]{1,0:T(8,128)(2,1)S(1)} collective-permute-done((bf16[64,1664]{1,0:T(8,128)(2,1)S(1)}, bf16[64,1664]{1,0:T(8,128)(2,1)S(1)}, u32[]{:S(2)}, u32[]{:S(2)}) %collective-permute-start.12) | collective-permute-done | bytes 213024 | tf_op jit(solution)/shard_map/ppermute | solution.py:407
  55.5 0.0 collective-permute-start.16
  55.5 0.0 collective-permute-done.8.refs_10_
  55.5 0.0 collective-permute-start.23
  55.5 0.0 collective-permute-done.17.refs_19_
  55.5 2.0 %collective-permute-start.20 = (bf16[2,8,32,128]{3,2,1,0:T(8,128)(2,1)S(1)}, bf16[2,8,32,128]{3,2,1,0:T(8,128)(2,1)S(1)}, u32[]{:S(2)}, u32[]{:S(2)}) collective-permute-start(bf16[2,8,32,128]{3,2,1,0:T(8,128)(2,1)S(1)} %collective-permute-done.19.refs_2_), channel_id=1, source_target_pairs={{0,1},{1,0},{2,3},{3,2},{4,5},{5,4},{6,7},{7,6},{8,9},{9,8},{10,11... | collective-permute-start | bytes 393224 | tf_op jit(solution)/shard_map/ppermute | solution.py:407
  57.6 0.0 collective-permute-done.15.refs_17_
  57.6 0.0 collective-permute-done.16.refs_18_
  57.6 3.0 %gather.1.dense = bf16[256,1664]{1,0:T(8,128)(2,1)S(1)} custom-call(s32[32]{0:T(128)S(1)} %bitcast_add_fusion.refs_0_, s32[32]{0:T(128)S(1)} %collective-permute-done.refs_1_, s32[32]{0:T(128)S(1)} %collective-permute-done.1.refs_2_, s32[32]{0:T(128)S(1)} %collective-permute-done.2.refs_3_, bf16[64,1664]{1,0:T(8,128)(2,1)S(1)} %get-tuple-element.14.refs_4_, ...), custom_call_target="tpu_custom_call" | custom-call | tf_op jit(solution)/shard_map/gather/pallas_call | solution.py:265
  60.6 1.3 %collective-permute-done.23.refs_3_ = bf16[2,8,32,128]{3,2,1,0:T(8,128)(2,1)S(1)} collective-permute-done((bf16[2,8,32,128]{3,2,1,0:T(8,128)(2,1)S(1)}, bf16[2,8,32,128]{3,2,1,0:T(8,128)(2,1)S(1)}, u32[]{:S(2)}, u32[]{:S(2)}) %collective-permute-start.23) | collective-permute-done | bytes 131104 | tf_op jit(solution)/shard_map/ppermute | solution.py:407
  61.9 0.0 collective-permute-done.18.refs_1_
  61.9 2.6 %convolve.3 = (f32[2,16,1536]{2,1,0:T(8,128)S(1)}, bf16[2,16,1536]{2,1,0:T(8,128)(2,1)S(1)}) custom-call(bf16[256,1664]{1,0:T(8,128)(2,1)S(1)} %gather.1.dense, bf16[4,8,32,128]{3,2,1,0:T(8,128)(2,1)S(1)} %get-tuple-element.16.refs_0_, bf16[4,8,32,128]{3,2,1,0:T(8,128)(2,1)S(1)} %collective-permute-done.18.refs_1_, ...), custom_call_target="tpu_custom_call" | custom-call | tf_op jit(solution)/shard_map/convolve/pallas_call | solution.py:351
  64.5 0.1 collective-permute-start.24
  64.6 0.0 collective-permute-done.20.refs_3_
  64.6 2.6 %convolve.2 = (f32[2,16,1536]{2,1,0:T(8,128)S(1)}, bf16[2,16,1536]{2,1,0:T(8,128)(2,1)S(1)}) custom-call(bf16[256,1664]{1,0:T(8,128)(2,1)S(1)} %gather.1.dense, bf16[4,8,32,128]{3,2,1,0:T(8,128)(2,1)S(1)} %get-tuple-element.16.refs_0_, bf16[4,8,32,128]{3,2,1,0:T(8,128)(2,1)S(1)} %collective-permute-done.18.refs_1_, ...), custom_call_target="tpu_custom_call" | custom-call | tf_op jit(solution)/shard_map/convolve/pallas_call | solution.py:351
  67.2 2.1 %collective-permute-start.21 = (bf16[2,16,1536]{2,1,0:T(8,128)(2,1)S(1)}, bf16[2,16,1536]{2,1,0:T(8,128)(2,1)S(1)}, u32[]{:S(2)}, u32[]{:S(2)}) collective-permute-start(bf16[2,16,1536]{2,1,0:T(8,128)(2,1)S(1)} %get-tuple-element.19), channel_id=1, source_target_pairs={{0,1},{1,0},{2,3},{3,2},{4,5},{5,4},{6,7},{7,6},{8,9},{9,8},{10,11... | collective-permute-start | bytes 294920 | tf_op jit(solution)/shard_map/ppermute | solution.py:407
  69.3 0.0 collective-permute-done.24.got_ref
  69.3 0.8 %assemble.2.refs_0_ = f32[4,3,16,1024]{3,2,1,0:T(8,128)} custom-call(f32[2,16,1536]{2,1,0:T(8,128)S(1)} %get-tuple-element.21.own_ref, bf16[2,16,1536]{2,1,0:T(8,128)(2,1)S(1)} %collective-permute-done.24.got_ref), custom_call_target="tpu_custom_call" | custom-call | tf_op jit(solution)/shard_map/assemble/pallas_call | solution.py:394
  70.0 1.8 %collective-permute-done.21.got_ref = bf16[2,16,1536]{2,1,0:T(8,128)(2,1)S(1)} collective-permute-done((bf16[2,16,1536]{2,1,0:T(8,128)(2,1)S(1)}, bf16[2,16,1536]{2,1,0:T(8,128)(2,1)S(1)}, u32[]{:S(2)}, u32[]{:S(2)}) %collective-permute-start.21) | collective-permute-done | bytes 98336 | tf_op jit(solution)/shard_map/ppermute | solution.py:407
  71.9 0.8 %assemble.3 = f32[4,3,16,1024]{3,2,1,0:T(8,128)} custom-call(f32[2,16,1536]{2,1,0:T(8,128)S(1)} %get-tuple-element.18.own_ref, bf16[2,16,1536]{2,1,0:T(8,128)(2,1)S(1)} %collective-permute-done.21.got_ref, f32[4,3,16,1024]{3,2,1,0:T(8,128)} %assemble.2.refs_0_), custom_call_target="tpu_custom_call", output_to_operand_aliasing={{}: (2, {})} | custom-call | tf_op jit(solution)/shard_map/assemble/pallas_call | solution.py:394
  (4 shorter events, 0.0 us)
Async XLA Ops:
  0.0 11.5 %copy-start.3 = (s32[32]{0:T(128)S(1)}, s32[32]{0:T(128)}, u32[]{:S(2)}) copy-start(s32[32]{0:T(128)} %param.8) | copy-start | bytes 388
  0.0 11.5 %copy-start.4 = (s32[32,1]{0,1:T(1,128)S(1)}, s32[32,1]{0,1:T(1,128)}, u32[]{:S(2)}) copy-start(s32[32,1]{0,1:T(1,128)} %param.7) | copy-start | bytes 388
  0.0 1.7 %copy-start = (bf16[64,6,3,1024]{3,0,2,1:T(8,128)(2,1)S(1)}, bf16[64,6,3,1024]{3,0,2,1:T(8,128)(2,1)}, u32[]{:S(2)}) copy-start(bf16[64,6,3,1024]{3,0,2,1:T(8,128)(2,1)} %param.5) | copy-start | bytes 7077892
  1.7 0.7 copy-start.2
  2.4 6.1 %copy-start.1 = (bf16[32,64,128]{2,1,0:T(8,128)(2,1)S(1)}, bf16[32,64,128]{2,1,0:T(8,128)(2,1)}, u32[]{:S(2)}) copy-start(bf16[32,64,128]{2,1,0:T(8,128)(2,1)} %slip_ref.1) | copy-start | bytes 1572868
  3.3 32.8 %collective-permute-start.5 = (bf16[64,1664]{1,0:T(8,128)(2,1)S(1)}, bf16[64,1664]{1,0:T(8,128)(2,1)S(1)}, u32[]{:S(2)}, u32[]{:S(2)}) collective-permute-start(bf16[64,1664]{1,0:T(8,128)(2,1)S(1)} %get-tuple-element.15), channel_id=1, source_target_pairs={{0,3},{1,2},{2,1},{3,0},{4,7},{5,6},{6,5},{7,4},{8,11},{9,10},{10,... | collective-permute-start | bytes 638984 | tf_op jit(solution)/shard_map/ppermute | solution.py:407
  11.4 23.5 %collective-permute-start.19 = (bf16[2,8,32,128]{3,2,1,0:T(8,128)(2,1)S(1)}, bf16[2,8,32,128]{3,2,1,0:T(8,128)(2,1)S(1)}, u32[]{:S(2)}, u32[]{:S(2)}) collective-permute-start(bf16[2,8,32,128]{3,2,1,0:T(8,128)(2,1)S(1)} %get-tuple-element.17), channel_id=1, source_target_pairs={{0,2},{1,3},{2,0},{3,1},{4,6},{5,7},{6,4},{7,5},{8,10},{9,11},{10,... | collective-permute-start | bytes 393224 | tf_op jit(solution)/shard_map/ppermute | solution.py:407
  11.5 5.5 %collective-permute-start.2 = (s32[32]{0:T(128)S(1)}, s32[32]{0:T(128)S(1)}, u32[]{:S(2)}, u32[]{:S(2)}) collective-permute-start(s32[32]{0:T(128)S(1)} %bitcast_add_fusion.refs_0_), channel_id=1, source_target_pairs={{0,3},{1,2},{2,1},{3,0},{4,7},{5,6},{6,5},{7,4},{8,11},{9,10},{10,... | collective-permute-start | bytes 392 | tf_op jit(solution)/shard_map/ppermute | solution.py:407
  13.4 21.4 %collective-permute-start.22 = (bf16[2,8,32,128]{3,2,1,0:T(8,128)(2,1)S(1)}, bf16[2,8,32,128]{3,2,1,0:T(8,128)(2,1)S(1)}, u32[]{:S(2)}, u32[]{:S(2)}) collective-permute-start(bf16[2,8,32,128]{3,2,1,0:T(8,128)(2,1)S(1)} %get-tuple-element.20), channel_id=1, source_target_pairs={{0,2},{1,3},{2,0},{3,1},{4,6},{5,7},{6,4},{7,5},{8,10},{9,11},{10,... | collective-permute-start | bytes 393224 | tf_op jit(solution)/shard_map/ppermute | solution.py:407
  14.5 14.4 %collective-permute-start.1 = (s32[32]{0:T(128)S(1)}, s32[32]{0:T(128)S(1)}, u32[]{:S(2)}, u32[]{:S(2)}) collective-permute-start(s32[32]{0:T(128)S(1)} %bitcast_add_fusion.refs_0_), channel_id=1, source_target_pairs={{0,2},{1,3},{2,0},{3,1},{4,6},{5,7},{6,4},{7,5},{8,10},{9,11},{10,... | collective-permute-start | bytes 392 | tf_op jit(solution)/shard_map/ppermute | solution.py:407
  17.0 19.7 %collective-permute-start.3 = (bf16[64,1664]{1,0:T(8,128)(2,1)S(1)}, bf16[64,1664]{1,0:T(8,128)(2,1)S(1)}, u32[]{:S(2)}, u32[]{:S(2)}) collective-permute-start(bf16[64,1664]{1,0:T(8,128)(2,1)S(1)} %get-tuple-element.15), channel_id=1, source_target_pairs={{0,1},{1,0},{2,3},{3,2},{4,5},{5,4},{6,7},{7,6},{8,9},{9,8},{10,11... | collective-permute-start | bytes 638984 | tf_op jit(solution)/shard_map/ppermute | solution.py:407
  28.9 4.5 %collective-permute-start = (s32[32]{0:T(128)S(1)}, s32[32]{0:T(128)S(1)}, u32[]{:S(2)}, u32[]{:S(2)}) collective-permute-start(s32[32]{0:T(128)S(1)} %bitcast_add_fusion.refs_0_), channel_id=1, source_target_pairs={{0,1},{1,0},{2,3},{3,2},{4,5},{5,4},{6,7},{7,6},{8,9},{9,8},{10,11... | collective-permute-start | bytes 392 | tf_op jit(solution)/shard_map/ppermute | solution.py:407
  33.4 8.1 %collective-permute-start.10 = (bf16[64,1664]{1,0:T(8,128)(2,1)S(1)}, bf16[64,1664]{1,0:T(8,128)(2,1)S(1)}, u32[]{:S(2)}, u32[]{:S(2)}) collective-permute-start(bf16[64,1664]{1,0:T(8,128)(2,1)S(1)} %get-tuple-element.14.refs_4_), channel_id=1, source_target_pairs={{0,8},{4,12},{8,0},{12,4},{1,9},{5,13},{9,1},{13,5},{2,10},{6,14},... | collective-permute-start | bytes 638984 | tf_op jit(solution)/shard_map/ppermute | solution.py:407
  34.9 8.1 %collective-permute-start.6 = (bf16[64,1664]{1,0:T(8,128)(2,1)S(1)}, bf16[64,1664]{1,0:T(8,128)(2,1)S(1)}, u32[]{:S(2)}, u32[]{:S(2)}) collective-permute-start(bf16[64,1664]{1,0:T(8,128)(2,1)S(1)} %get-tuple-element.14.refs_4_), channel_id=1, source_target_pairs={{0,4},{4,0},{8,12},{12,8},{1,5},{5,1},{9,13},{13,9},{2,6},{6,2},{1... | collective-permute-start | bytes 638984 | tf_op jit(solution)/shard_map/ppermute | solution.py:407
  34.9 13.0 %collective-permute-start.4 = (bf16[64,1664]{1,0:T(8,128)(2,1)S(1)}, bf16[64,1664]{1,0:T(8,128)(2,1)S(1)}, u32[]{:S(2)}, u32[]{:S(2)}) collective-permute-start(bf16[64,1664]{1,0:T(8,128)(2,1)S(1)} %get-tuple-element.14.refs_4_), channel_id=1, source_target_pairs={{0,2},{1,3},{2,0},{3,1},{4,6},{5,7},{6,4},{7,5},{8,10},{9,11},{10,... | collective-permute-start | bytes 638984 | tf_op jit(solution)/shard_map/ppermute | solution.py:407
  36.1 11.8 %collective-permute-start.13 = (bf16[64,1664]{1,0:T(8,128)(2,1)S(1)}, bf16[64,1664]{1,0:T(8,128)(2,1)S(1)}, u32[]{:S(2)}, u32[]{:S(2)}) collective-permute-start(bf16[64,1664]{1,0:T(8,128)(2,1)S(1)} %collective-permute-done.5.refs_7_), channel_id=1, source_target_pairs={{0,8},{4,12},{8,0},{12,4},{1,9},{5,13},{9,1},{13,5},{2,10},{6,14},... | collective-permute-start | bytes 638984 | tf_op jit(solution)/shard_map/ppermute | solution.py:407
  36.7 11.8 %collective-permute-start.9 = (bf16[64,1664]{1,0:T(8,128)(2,1)S(1)}, bf16[64,1664]{1,0:T(8,128)(2,1)S(1)}, u32[]{:S(2)}, u32[]{:S(2)}) collective-permute-start(bf16[64,1664]{1,0:T(8,128)(2,1)S(1)} %collective-permute-done.5.refs_7_), channel_id=1, source_target_pairs={{0,4},{4,0},{8,12},{12,8},{1,5},{5,1},{9,13},{13,9},{2,6},{6,2},{1... | collective-permute-start | bytes 638984 | tf_op jit(solution)/shard_map/ppermute | solution.py:407
  41.5 8.0 %collective-permute-start.11 = (bf16[64,1664]{1,0:T(8,128)(2,1)S(1)}, bf16[64,1664]{1,0:T(8,128)(2,1)S(1)}, u32[]{:S(2)}, u32[]{:S(2)}) collective-permute-start(bf16[64,1664]{1,0:T(8,128)(2,1)S(1)} %collective-permute-done.3.refs_5_), channel_id=1, source_target_pairs={{0,8},{4,12},{8,0},{12,4},{1,9},{5,13},{9,1},{13,5},{2,10},{6,14},... | collective-permute-start | bytes 638984 | tf_op jit(solution)/shard_map/ppermute | solution.py:407
  43.0 6.5 %collective-permute-start.7 = (bf16[64,1664]{1,0:T(8,128)(2,1)S(1)}, bf16[64,1664]{1,0:T(8,128)(2,1)S(1)}, u32[]{:S(2)}, u32[]{:S(2)}) collective-permute-start(bf16[64,1664]{1,0:T(8,128)(2,1)S(1)} %collective-permute-done.3.refs_5_), channel_id=1, source_target_pairs={{0,4},{4,0},{8,12},{12,8},{1,5},{5,1},{9,13},{13,9},{2,6},{6,2},{1... | collective-permute-start | bytes 638984 | tf_op jit(solution)/shard_map/ppermute | solution.py:407
  47.8 2.0 %collective-permute-start.14 = (bf16[64,1664]{1,0:T(8,128)(2,1)S(1)}, bf16[64,1664]{1,0:T(8,128)(2,1)S(1)}, u32[]{:S(2)}, u32[]{:S(2)}) collective-permute-start(bf16[64,1664]{1,0:T(8,128)(2,1)S(1)} %collective-permute-done.10.refs_12_), channel_id=1, source_target_pairs={{0,4},{4,0},{8,12},{12,8},{1,5},{5,1},{9,13},{13,9},{2,6},{6,2},{1... | collective-permute-start | bytes 638984 | tf_op jit(solution)/shard_map/ppermute | solution.py:407
  47.9 7.6 %collective-permute-start.12 = (bf16[64,1664]{1,0:T(8,128)(2,1)S(1)}, bf16[64,1664]{1,0:T(8,128)(2,1)S(1)}, u32[]{:S(2)}, u32[]{:S(2)}) collective-permute-start(bf16[64,1664]{1,0:T(8,128)(2,1)S(1)} %collective-permute-done.4.refs_6_), channel_id=1, source_target_pairs={{0,8},{4,12},{8,0},{12,4},{1,9},{5,13},{9,1},{13,5},{2,10},{6,14},... | collective-permute-start | bytes 638984 | tf_op jit(solution)/shard_map/ppermute | solution.py:407
  48.5 7.1 %collective-permute-start.8 = (bf16[64,1664]{1,0:T(8,128)(2,1)S(1)}, bf16[64,1664]{1,0:T(8,128)(2,1)S(1)}, u32[]{:S(2)}, u32[]{:S(2)}) collective-permute-start(bf16[64,1664]{1,0:T(8,128)(2,1)S(1)} %collective-permute-done.4.refs_6_), channel_id=1, source_target_pairs={{0,4},{4,0},{8,12},{12,8},{1,5},{5,1},{9,13},{13,9},{2,6},{6,2},{1... | collective-permute-start | bytes 638984 | tf_op jit(solution)/shard_map/ppermute | solution.py:407
  49.5 6.1 %collective-permute-start.17 = (bf16[64,1664]{1,0:T(8,128)(2,1)S(1)}, bf16[64,1664]{1,0:T(8,128)(2,1)S(1)}, u32[]{:S(2)}, u32[]{:S(2)}) collective-permute-start(bf16[64,1664]{1,0:T(8,128)(2,1)S(1)} %collective-permute-done.13.refs_15_), channel_id=1, source_target_pairs={{0,4},{4,0},{8,12},{12,8},{1,5},{5,1},{9,13},{13,9},{2,6},{6,2},{1... | collective-permute-start | bytes 638984 | tf_op jit(solution)/shard_map/ppermute | solution.py:407
  49.5 12.4 %collective-permute-start.18 = (bf16[4,8,32,128]{3,2,1,0:T(8,128)(2,1)S(1)}, bf16[4,8,32,128]{3,2,1,0:T(8,128)(2,1)S(1)}, u32[]{:S(2)}, u32[]{:S(2)}) collective-permute-start(bf16[4,8,32,128]{3,2,1,0:T(8,128)(2,1)S(1)} %get-tuple-element.16.refs_0_), channel_id=1, source_target_pairs={{0,1},{1,0},{2,3},{3,2},{4,5},{5,4},{6,7},{7,6},{8,9},{9,8},{10,11... | collective-permute-start | bytes 786440 | tf_op jit(solution)/shard_map/ppermute | solution.py:407
  49.9 7.7 %collective-permute-start.15 = (bf16[64,1664]{1,0:T(8,128)(2,1)S(1)}, bf16[64,1664]{1,0:T(8,128)(2,1)S(1)}, u32[]{:S(2)}, u32[]{:S(2)}) collective-permute-start(bf16[64,1664]{1,0:T(8,128)(2,1)S(1)} %collective-permute-done.11.refs_13_), channel_id=1, source_target_pairs={{0,4},{4,0},{8,12},{12,8},{1,5},{5,1},{9,13},{13,9},{2,6},{6,2},{1... | collective-permute-start | bytes 638984 | tf_op jit(solution)/shard_map/ppermute | solution.py:407
  55.5 2.0 %collective-permute-start.16 = (bf16[64,1664]{1,0:T(8,128)(2,1)S(1)}, bf16[64,1664]{1,0:T(8,128)(2,1)S(1)}, u32[]{:S(2)}, u32[]{:S(2)}) collective-permute-start(bf16[64,1664]{1,0:T(8,128)(2,1)S(1)} %collective-permute-done.12.refs_14_), channel_id=1, source_target_pairs={{0,4},{4,0},{8,12},{12,8},{1,5},{5,1},{9,13},{13,9},{2,6},{6,2},{1... | collective-permute-start | bytes 638984 | tf_op jit(solution)/shard_map/ppermute | solution.py:407
  55.5 6.4 %collective-permute-start.23 = (bf16[2,8,32,128]{3,2,1,0:T(8,128)(2,1)S(1)}, bf16[2,8,32,128]{3,2,1,0:T(8,128)(2,1)S(1)}, u32[]{:S(2)}, u32[]{:S(2)}) collective-permute-start(bf16[2,8,32,128]{3,2,1,0:T(8,128)(2,1)S(1)} %collective-permute-done.22.refs_2_), channel_id=1, source_target_pairs={{0,1},{1,0},{2,3},{3,2},{4,5},{5,4},{6,7},{7,6},{8,9},{9,8},{10,11... | collective-permute-start | bytes 393224 | tf_op jit(solution)/shard_map/ppermute | solution.py:407
  55.5 9.0 %collective-permute-start.20 = (bf16[2,8,32,128]{3,2,1,0:T(8,128)(2,1)S(1)}, bf16[2,8,32,128]{3,2,1,0:T(8,128)(2,1)S(1)}, u32[]{:S(2)}, u32[]{:S(2)}) collective-permute-start(bf16[2,8,32,128]{3,2,1,0:T(8,128)(2,1)S(1)} %collective-permute-done.19.refs_2_), channel_id=1, source_target_pairs={{0,1},{1,0},{2,3},{3,2},{4,5},{5,4},{6,7},{7,6},{8,9},{9,8},{10,11... | collective-permute-start | bytes 393224 | tf_op jit(solution)/shard_map/ppermute | solution.py:407
  64.5 4.8 %collective-permute-start.24 = (bf16[2,16,1536]{2,1,0:T(8,128)(2,1)S(1)}, bf16[2,16,1536]{2,1,0:T(8,128)(2,1)S(1)}, u32[]{:S(2)}, u32[]{:S(2)}) collective-permute-start(bf16[2,16,1536]{2,1,0:T(8,128)(2,1)S(1)} %get-tuple-element.22), channel_id=1, source_target_pairs={{0,1},{1,0},{2,3},{3,2},{4,5},{5,4},{6,7},{7,6},{8,9},{9,8},{10,11... | collective-permute-start | bytes 294920 | tf_op jit(solution)/shard_map/ppermute | solution.py:407
  67.2 4.7 %collective-permute-start.21 = (bf16[2,16,1536]{2,1,0:T(8,128)(2,1)S(1)}, bf16[2,16,1536]{2,1,0:T(8,128)(2,1)S(1)}, u32[]{:S(2)}, u32[]{:S(2)}) collective-permute-start(bf16[2,16,1536]{2,1,0:T(8,128)(2,1)S(1)} %get-tuple-element.19), channel_id=1, source_target_pairs={{0,1},{1,0},{2,3},{3,2},{4,5},{5,4},{6,7},{7,6},{8,9},{9,8},{10,11... | collective-permute-start | bytes 294920 | tf_op jit(solution)/shard_map/ppermute | solution.py:407

commit v2 on v1

--- a/solution.py
+++ b/solution.py
@@ -95,7 +95,7 @@
 
     for step in range(steps):
         copy(step).start()
-    mech_scratch[...] = jnp.transpose(mech_ref[...].astype(F32))
+    mech_scratch[...] = jnp.transpose(mech_ref[...])
     half = samples // 2
     parity = lax.rem(lax.axis_index("worker"), 2)
 
@@ -146,7 +146,7 @@
         ],
         compiler_params=pltpu.CompilerParams(vmem_limit_bytes=8 * MIB),
         name="combine",
-    )(jnp.transpose(sgt, (1, 2, 0, 3)), mechanism)
+    )(jnp.transpose(sgt, (1, 2, 0, 3)), mechanism.astype(F32))
 
 
 def group_transpose(rows, lane):
@@ -221,49 +221,63 @@
     )(slip)
 
 
-def gather_kernel(sources, *refs):
-    codes, green, dense, hot = refs[:sources], refs[sources:-2], refs[-2], refs[-1]
-    pieces = len(green)
-    points, width = green[0].shape
-    blocks_here = points // BLK
+def hot_rows(hot, codes, slots, picks, points, here):
     requests = codes[0].shape[0] // RUP_SLOTS
-    handler, worker = lax.axis_index("handler"), lax.axis_index("worker")
     tall = requests * BLK
-    span = 2 * LANES
     row = lax.broadcasted_iota(jnp.int32, (tall, LANES), 0)
     lane = lax.broadcasted_iota(jnp.int32, (tall, LANES), 1)
-    for slot in range(RUP_SLOTS):
-        for j in range(sources):
-            asked = jnp.zeros((tall, LANES), jnp.int32)
+    per = LANES // points
+    columns = []
+    for p in range(0, len(picks), per):
+        column = lane + (picks[p] * points)
+        for q in range(1, per):
+            column = jnp.where(lane >= q * points, lane + (picks[p + q] - q) * points, column)
+        columns.append(column - row)
+    for index, slot in enumerate(slots):
+        for j, code in enumerate(codes):
+            asked = None
             for n in range(requests):
-                code = codes[j][slot * requests + n]
-                owner = code // blocks_here
-                piece = ((owner // sources) ^ handler) * sources + (lax.rem(owner, sources) ^ worker)
-                base = piece * points + lax.rem(code, blocks_here) * BLK - n * BLK
-                asked = jnp.where(row >= n * BLK, base, asked)
-            asked = asked + row - lane
-            put = (slot * sources + j) * tall
-            for c in range(0, pieces * points, LANES):
-                hot[put : put + tall, c : c + LANES] = jnp.where(asked == c, 1.0, 0.0).astype(BF)
-    together = max(1, span // points)
-    for c in range(0, width, span):
-        e = min(width, c + span)
-        total = None
-        for p in range(0, pieces, together):
-            block = jnp.concatenate([g[:, c:e] for g in green[p : p + together]], axis=0)
-            part = jnp.dot(
-                hot[:, p * points : (p + together) * points], block, preferred_element_type=F32
-            )
-            total = part if total is None else total + part
-        dense[:, c:e] = total.astype(BF)
-
-
-def gather(codes, green):
+                base = (code[slot * requests + n] ^ here) - n * BLK
+                asked = jnp.full((tall, LANES), base) if n == 0 else jnp.where(row >= n * BLK, base, asked)
+            put = (index * len(codes) + j) * tall
+            for c, column in enumerate(columns):
+                hot[put : put + tall, c * LANES : (c + 1) * LANES] = jnp.where(
+                    asked == column, 1.0, 0.0
+                ).astype(BF)
+
+
+def picked(hot, green, lo, hi):
+    points = green[0].shape[0]
+    together = max(1, 2 * LANES // points)
+    total = None
+    for p in range(0, len(green), together):
+        block = jnp.concatenate([g[:, lo:hi] for g in green[p : p + together]], axis=0)
+        part = jnp.dot(
+            hot[:, p * points : (p + together) * points], block, preferred_element_type=F32
+        )
+        total = part if total is None else total + part
+    return total
+
+
+def my_place(workers, points):
+    return (lax.axis_index("handler") * workers + lax.axis_index("worker")) * points
+
+
+def gather_kernel(sources, picks, *refs):
+    codes, green, dense, hot = refs[:sources], refs[sources:-2], refs[-2], refs[-1]
+    points, width = green[0].shape
+    hot_rows(hot, codes, range(RUP_SLOTS), picks, points, my_place(sources, points))
+    for c in range(0, width, 2 * LANES):
+        e = min(width, c + 2 * LANES)
+        dense[:, c:e] = picked(hot, green, c, e).astype(BF)
+
+
+def gather(codes, picks, green):
     points, width = green[0].shape
     asked = len(codes) * codes[0].shape[0] * BLK
     vmem = pl.BlockSpec(memory_space=pltpu.VMEM)
     return pl.pallas_call(
-        functools.partial(gather_kernel, len(codes)),
+        functools.partial(gather_kernel, len(codes), picks),
         in_specs=[pl.BlockSpec(memory_space=pltpu.SMEM)] * len(codes) + [vmem] * len(green),
         out_specs=vmem,
         out_shape=jax.ShapeDtypeStruct((asked, width), BF),
@@ -273,46 +287,57 @@
     )(*codes, *green)
 
 
-def convolve_kernel(base, dense, *refs):
-    slips = refs[:-5]
-    own_ref, send_ref, left, right, product = refs[-5:]
-    sources = len(slips)
-    width = dense.shape[1]
+def convolve_kernel(base, picks, sources, *refs):
+    codes, given, refs = refs[:sources], refs[sources], refs[sources + 1 :]
+    green, refs = refs[: len(picks)], refs[len(picks) :]
+    slips, refs = refs[:sources], refs[sources:]
+    own_ref, send_ref, hot, dense, left, right, product = refs
+    points, width = green[0].shape
     slots = own_ref.shape[0]
     _, coarse, group, _ = slips[0].shape
-    per_source = dense.shape[0] // (RUP_SLOTS * sources)
+    asked = given.shape[0] // RUP_SLOTS
+    per_source = asked // sources
     tiles = width // LANES
     samples = (width - LANES) * 2 // 3
     first = samples // LANES
     parity = lax.rem(lax.axis_index("worker"), 2)
     span = 2 * LANES
+
+    hot_rows(hot, codes, range(base, base + slots), picks, points, my_place(sources, points))
+    for c in range(0, width, span):
+        e = min(width, c + span)
+        had = given[base * asked : (base + slots) * asked, c:e].astype(F32)
+        dense[:, c:e] = (had + picked(hot, green, c, e)).astype(BF)
+
     lane = lax.broadcasted_iota(jnp.int32, (SUB, LANES), 1)
     wide_lane = lax.broadcasted_iota(jnp.int32, (per_source, LANES), 1)
     zero = jnp.zeros((SUB, LANES), F32)
 
-    def slot_body(slot, carry):
+    for slot in range(slots):
         for j in range(sources):
             for a in range(coarse):
-                left[a * group : (a + 1) * group, j * LANES : (j + 1) * LANES] = slips[j][
+                left[slot, a * group : (a + 1) * group, j * LANES : (j + 1) * LANES] = slips[j][
                     slot + (base if slips[j].shape[0] > slots else 0), a
                 ]
-            at = pl.multiple_of(((base + slot) * sources + j) * per_source, per_source)
+            at = (slot * sources + j) * per_source
             for b in range(SUB):
                 put = j * LANES + b * per_source
                 before = jnp.zeros((per_source, LANES), BF)
                 for m in range(tiles):
-                    value = dense[pl.ds(at, per_source), m * LANES : (m + 1) * LANES]
+                    value = dense[at : at + per_source, m * LANES : (m + 1) * LANES]
                     if b:
                         turn = pltpu.roll(value, b, 1)
                         if m == first:
                             before = jnp.zeros((per_source, LANES), BF)
                         value = jnp.where(wide_lane < b, before, turn)
                         before = turn
-                    right[put : put + per_source, m * LANES : (m + 1) * LANES] = value
+                    right[slot, put : put + per_source, m * LANES : (m + 1) * LANES] = value
 
         for c in range(0, width, span):
             e = min(width, c + span)
-            product[:, c:e] = jnp.dot(left[...], right[:, c:e], preferred_element_type=F32)
+            product[slot, :, c:e] = jnp.dot(
+                left[slot], right[slot, :, c:e], preferred_element_type=F32
+            )
 
         for side in range(2):
             for u in range(0, group // 2, SUB):
@@ -323,7 +348,7 @@
                     )
                     before = zero
                     for m in range(tiles):
-                        value = product[pl.ds(start, SUB), m * LANES : (m + 1) * LANES]
+                        value = product[slot, pl.ds(start, SUB), m * LANES : (m + 1) * LANES]
                         if a:
                             value = pltpu.roll(value, a * SUB, 1)
                         if m == first:
@@ -337,33 +362,34 @@
                         own_ref[slot, u : u + SUB, m * LANES : (m + 1) * LANES] = value
                     else:
                         send_ref[slot, u : u + SUB, m * LANES : (m + 1) * LANES] = value.astype(BF)
-        return carry
-
-    lax.fori_loop(0, slots, slot_body, 0)
-
-
-def convolve(base, dense, slips):
-    width = dense.shape[1]
+
+
+def convolve(base, codes, given, picks, green, slips):
+    points, width = green[0].shape
     slots = slips[-1].shape[0]
     _, coarse, group, depth = slips[0].shape
     inner = depth * len(slips)
+    asked = given.shape[0] // RUP_SLOTS * slots
     vmem = pl.BlockSpec(memory_space=pltpu.VMEM)
+    smem = pl.BlockSpec(memory_space=pltpu.SMEM)
     return pl.pallas_call(
-        functools.partial(convolve_kernel, base),
-        in_specs=[vmem] * (1 + len(slips)),
+        functools.partial(convolve_kernel, base, picks, len(slips)),
+        in_specs=[smem] * len(codes) + [vmem] * (1 + len(green) + len(slips)),
         out_specs=[vmem, vmem],
         out_shape=[
             jax.ShapeDtypeStruct((slots, group // 2, width - LANES), F32),
             jax.ShapeDtypeStruct((slots, group // 2, width - LANES), BF),
         ],
         scratch_shapes=[
-            pltpu.VMEM((coarse * group, inner), BF),
-            pltpu.VMEM((inner, width), BF),
-            pltpu.VMEM((coarse * group, width), F32),
+            pltpu.VMEM((asked, len(green) * points), BF),
+            pltpu.VMEM((asked, width), BF),
+            pltpu.VMEM((slots, coarse * group, inner), BF),
+            pltpu.VMEM((slots, inner, width), BF),
+            pltpu.VMEM((slots, coarse * group, width), F32),
         ],
-        compiler_params=pltpu.CompilerParams(vmem_limit_bytes=12 * MIB),
+        compiler_params=pltpu.CompilerParams(vmem_limit_bytes=16 * MIB),
         name="convolve",
-    )(dense, *slips)
+    )(*codes, given, *green, *slips)
 
 
 def assemble_kernel(own_ref, got_ref, *refs):
@@ -412,7 +438,7 @@
     points, _, _, samples = sgt.shape
     same, other = combine(sgt, mechanism)
 
-    code = req_owner[:, 0] * (points // BLK) + req_local
+    code = req_owner[:, 0] * points + req_local * BLK
     codes = [code] + [swap(code, "worker", flip) for flip in range(1, workers)]
 
     green = {(0, 0): same}
@@ -423,7 +449,10 @@
         for (hand, flip), value in list(green.items()):
             green[hand ^ bit, flip] = swap(value, "handler", bit)
         bit //= 2
-    dense = gather(codes, [green[hand, flip] for hand in range(handlers) for flip in range(workers)])
+    last = [hand * workers + workers - 1 for hand in range(handlers)]
+    early = [pick for pick in range(handlers * workers) if pick not in last]
+    piece = [green[divmod(pick, workers)] for pick in range(handlers * workers)]
+    given = gather(codes, early, [piece[pick] for pick in early])
 
     turned = turn_slip(slip, workers)
     near = [turned[0], swap(turned[0], "worker", 1)]
@@ -435,7 +464,9 @@
             value = turned[1 + (flip // 2 - 1) * PARTS + part]
             slips.append(swap(value, "worker", flip))
             slips.append(swap(slips[-1], "worker", 1))
-        own, send = convolve(part * RUP_SLOTS // PARTS, dense, slips)
+        own, send = convolve(
+            part * RUP_SLOTS // PARTS, codes, given, last, [piece[pick] for pick in last], slips
+        )
         results.append((own, swap(send, "worker", 1)))
     for part, (own, got) in enumerate(results):
         out = assemble(part * RUP_SLOTS // PARTS, own, got, samples, out)
@@ -452,7 +483,10 @@
         handlers * workers * points * width * 4 <= VMEM_BUDGET
         and power_of_two(handlers)
         and power_of_two(workers)
+        and power_of_two(points)
+        and points <= LANES
         and workers >= 2
+        and handlers * points % LANES == 0
         and kinds == 3
         and samples % (2 * LANES) == 0
         and depth == BLK * TAPS == LANES

time: 72.8 us -> 73.9 us (1.015)
  waiting for transfers between devices: 25.7 us -> 29.8 us
  starting transfers between devices: 30.9 us -> 27.5 us
    ppermute x25, waiting for transfers between devices: 25.7 us -> 29.8 us  [swap(): lax.ppermute(value, axis, [(i, i ^ flip) for i in range(lax.axis_size(axi...]
    ppermute x25, starting transfers between devices: 30.9 us -> 27.5 us  [swap(): lax.ppermute(value, axis, [(i, i ^ flip) for i in range(lax.axis_size(axi...]
    unnamed x10 -> x8, local copies, waits for them, and re-layouts: 2.38 us -> 1.68 us
  transfers between devices with their start and end apart: 25 -> 25, of which waited for: 9 -> 10; matrix products, arithmetic and copies ran while one was open for 0% -> 0% of each run, Pallas kernels for 16% -> 17%
where the time goes in v2:
time: 73.9 us; the launch traced here: 73.7 us
  waiting for transfers between devices  29.8 us (40%)
  starting transfers between devices  27.5 us (37%)
  Pallas kernels  13.9 us (19%)
  local copies, waits for them, and re-layouts  1.68 us (2%)
    ppermute x25, waiting for transfers between devices, swap(): lax.ppermute(value, axis, [(i, i ^ flip) for i in range(lax.axis_size(axi...  29.8 us
    ppermute x25, starting transfers between devices, swap(): lax.ppermute(value, axis, [(i, i ^ flip) for i in range(lax.axis_size(axi...  27.5 us
    pallas_call x2, Pallas kernels, convolve(): pl.pallas_call(functools.partial(convolve_kernel, base, picks, len(slips)...  7.07 us
    pallas_call x1, Pallas kernels, turn_slip(): pl.pallas_call(turn_kernel, in_specs=[vmem], out_specs=[vmem] * len(outs)...  2.9 us
    unnamed x8, local copies, waits for them, and re-layouts  1.68 us
    pallas_call x2, Pallas kernels, assemble(): pl.pallas_call(assemble_kernel, grid=(slots,), in_specs=[spec, spec] + [p...  1.52 us
    pallas_call x1, Pallas kernels, gather(): pl.pallas_call(functools.partial(gather_kernel, len(codes), picks), in_sp...  1.51 us
  transfers between devices with their start and end apart: 25, of which 10 were waited for; matrix products, arithmetic and copies ran while one was open for 0% of the time, Pallas kernels for 17%

profile of v2, /device:TPU:0, one launch (start us, length us, event | category | flops | bytes accessed | tf_op | source)
XLA Modules:
  0.0 73.7 jit_solution(2754034965606319671)
XLA Ops:
  0.0 0.0 copy-start.3
  0.0 0.0 copy-start.2
  0.0 0.7 convert_element_type.3.mech_ref
  0.7 1.7 %copy-done = bf16[64,6,3,1024]{3,0,2,1:T(8,128)(2,1)S(1)} copy-done((bf16[64,6,3,1024]{3,0,2,1:T(8,128)(2,1)S(1)}, bf16[64,6,3,1024]{3,0,2,1:T(8,128)(2,1)}, u32[]{:S(2)}) %copy-start) | copy-done | bytes 2359320
  2.4 0.9 %combine.1 = (bf16[64,1664]{1,0:T(8,128)(2,1)S(1)}, bf16[64,1664]{1,0:T(8,128)(2,1)S(1)}) custom-call(bf16[6,3,64,1024]{3,2,1,0:T(8,128)(2,1)S(1)} %bitcast.4, f32[6,64]{1,0:T(8,128)S(1)} %convert_element_type.3.mech_ref), custom_call_target="tpu_custom_call" | custom-call | tf_op jit(solution)/shard_map/combine/pallas_call | solution.py:137
  3.3 4.1 %collective-permute-start.4 = (bf16[64,1664]{1,0:T(8,128)(2,1)S(1)}, bf16[64,1664]{1,0:T(8,128)(2,1)S(1)}, u32[]{:S(2)}, u32[]{:S(2)}) collective-permute-start(bf16[64,1664]{1,0:T(8,128)(2,1)S(1)} %get-tuple-element.14.refs_4_), channel_id=1, source_target_pairs={{0,2},{1,3},{2,0},{3,1},{4,6},{5,7},{6,4},{7,5},{8,10},{9,11},{10,... | collective-permute-start | bytes 638984 | tf_op jit(solution)/shard_map/ppermute | solution.py:433
  7.5 0.0 copy-done.1
  7.5 2.9 %turn_slip.1 = (bf16[4,8,32,128]{3,2,1,0:T(8,128)(2,1)S(1)}, bf16[2,8,32,128]{3,2,1,0:T(8,128)(2,1)S(1)}, bf16[2,8,32,128]{3,2,1,0:T(8,128)(2,1)S(1)}) custom-call(bf16[32,64,128]{2,1,0:T(8,128)(2,1)S(1)} %copy-done.1), custom_call_target="tpu_custom_call" | custom-call | tf_op jit(solution)/shard_map/turn_slip/pallas_call | solution.py:213
  10.4 0.1 collective-permute-start.22
  10.5 0.0 copy-done.3
  10.5 0.0 copy-done.2
  10.5 1.9 %collective-permute-start = (s32[32]{0:T(128)S(1)}, s32[32]{0:T(128)S(1)}, u32[]{:S(2)}, u32[]{:S(2)}) collective-permute-start(s32[32]{0:T(128)S(1)} %bitcast_add_fusion.refs_0_), channel_id=1, source_target_pairs={{0,1},{1,0},{2,3},{3,2},{4,5},{5,4},{6,7},{7,6},{8,9},{9,8},{10,11... | collective-permute-start | bytes 392 | tf_op jit(solution)/shard_map/ppermute | solution.py:433
  12.4 2.6 %collective-permute-start.1 = (s32[32]{0:T(128)S(1)}, s32[32]{0:T(128)S(1)}, u32[]{:S(2)}, u32[]{:S(2)}) collective-permute-start(s32[32]{0:T(128)S(1)} %bitcast_add_fusion.refs_0_), channel_id=1, source_target_pairs={{0,2},{1,3},{2,0},{3,1},{4,6},{5,7},{6,4},{7,5},{8,10},{9,11},{10,... | collective-permute-start | bytes 392 | tf_op jit(solution)/shard_map/ppermute | solution.py:433
  15.0 0.5 collective-permute-start.3
  15.5 0.0 collective-permute-done.refs_1_
  15.5 3.7 %collective-permute-start.19 = (bf16[2,8,32,128]{3,2,1,0:T(8,128)(2,1)S(1)}, bf16[2,8,32,128]{3,2,1,0:T(8,128)(2,1)S(1)}, u32[]{:S(2)}, u32[]{:S(2)}) collective-permute-start(bf16[2,8,32,128]{3,2,1,0:T(8,128)(2,1)S(1)} %get-tuple-element.17), channel_id=1, source_target_pairs={{0,2},{1,3},{2,0},{3,1},{4,6},{5,7},{6,4},{7,5},{8,10},{9,11},{10,... | collective-permute-start | bytes 393224 | tf_op jit(solution)/shard_map/ppermute | solution.py:433
  19.2 7.6 %collective-permute-done.1.refs_2_ = s32[32]{0:T(128)S(1)} collective-permute-done((s32[32]{0:T(128)S(1)}, s32[32]{0:T(128)S(1)}, u32[]{:S(2)}, u32[]{:S(2)}) %collective-permute-start.1) | collective-permute-done | bytes 160 | tf_op jit(solution)/shard_map/ppermute | solution.py:433
  26.8 2.7 %collective-permute-start.2 = (s32[32]{0:T(128)S(1)}, s32[32]{0:T(128)S(1)}, u32[]{:S(2)}, u32[]{:S(2)}) collective-permute-start(s32[32]{0:T(128)S(1)} %bitcast_add_fusion.refs_0_), channel_id=1, source_target_pairs={{0,3},{1,2},{2,1},{3,0},{4,7},{5,6},{6,5},{7,4},{8,11},{9,10},{10,... | collective-permute-start | bytes 392 | tf_op jit(solution)/shard_map/ppermute | solution.py:433
  29.5 2.7 %collective-permute-done.2.refs_3_ = s32[32]{0:T(128)S(1)} collective-permute-done((s32[32]{0:T(128)S(1)}, s32[32]{0:T(128)S(1)}, u32[]{:S(2)}, u32[]{:S(2)}) %collective-permute-start.2) | collective-permute-done | bytes 160 | tf_op jit(solution)/shard_map/ppermute | solution.py:433
  32.2 1.8 %collective-permute-start.8 = (bf16[64,1664]{1,0:T(8,128)(2,1)S(1)}, bf16[64,1664]{1,0:T(8,128)(2,1)S(1)}, u32[]{:S(2)}, u32[]{:S(2)}) collective-permute-start(bf16[64,1664]{1,0:T(8,128)(2,1)S(1)} %get-tuple-element.14.refs_4_), channel_id=1, source_target_pairs={{0,8},{4,12},{8,0},{12,4},{1,9},{5,13},{9,1},{13,5},{2,10},{6,14},... | collective-permute-start | bytes 638984 | tf_op jit(solution)/shard_map/ppermute | solution.py:433
  34.0 0.0 collective-permute-done.22.refs_11_
  34.0 0.0 collective-permute-start.5
  34.0 0.0 collective-permute-done.19.refs_11_
  34.0 2.4 %collective-permute-start.14 = (bf16[64,1664]{1,0:T(8,128)(2,1)S(1)}, bf16[64,1664]{1,0:T(8,128)(2,1)S(1)}, u32[]{:S(2)}, u32[]{:S(2)}) collective-permute-start(bf16[64,1664]{1,0:T(8,128)(2,1)S(1)} %get-tuple-element.15), channel_id=1, source_target_pairs={{0,3},{1,2},{2,1},{3,0},{4,7},{5,6},{6,5},{7,4},{8,11},{9,10},{10,... | collective-permute-start | bytes 638984 | tf_op jit(solution)/shard_map/ppermute | solution.py:433
  36.4 0.0 collective-permute-done.4.refs_6_
  36.4 0.5 collective-permute-start.10
  37.0 0.0 collective-permute-done.3.refs_5_
  37.0 0.0 collective-permute-start.7
  37.0 1.0 %collective-permute-done.8.refs_10_ = bf16[64,1664]{1,0:T(8,128)(2,1)S(1)} collective-permute-done((bf16[64,1664]{1,0:T(8,128)(2,1)S(1)}, bf16[64,1664]{1,0:T(8,128)(2,1)S(1)}, u32[]{:S(2)}, u32[]{:S(2)}) %collective-permute-start.8) | collective-permute-done | bytes 213024 | tf_op jit(solution)/shard_map/ppermute | solution.py:433
  38.0 1.9 %collective-permute-start.9 = (bf16[64,1664]{1,0:T(8,128)(2,1)S(1)}, bf16[64,1664]{1,0:T(8,128)(2,1)S(1)}, u32[]{:S(2)}, u32[]{:S(2)}) collective-permute-start(bf16[64,1664]{1,0:T(8,128)(2,1)S(1)} %collective-permute-done.3.refs_5_), channel_id=1, source_target_pairs={{0,8},{4,12},{8,0},{12,4},{1,9},{5,13},{9,1},{13,5},{2,10},{6,14},... | collective-permute-start | bytes 638984 | tf_op jit(solution)/shard_map/ppermute | solution.py:433
  39.9 0.0 collective-permute-done.5.refs_7_
  39.9 0.0 collective-permute-start.11
  39.9 3.5 %collective-permute-done.14.refs_5_ = bf16[64,1664]{1,0:T(8,128)(2,1)S(1)} collective-permute-done((bf16[64,1664]{1,0:T(8,128)(2,1)S(1)}, bf16[64,1664]{1,0:T(8,128)(2,1)S(1)}, u32[]{:S(2)}, u32[]{:S(2)}) %collective-permute-start.14) | collective-permute-done | bytes 213024 | tf_op jit(solution)/shard_map/ppermute | solution.py:433
  43.4 0.0 collective-permute-start.6
  43.4 1.1 %collective-permute-done.10.refs_12_ = bf16[64,1664]{1,0:T(8,128)(2,1)S(1)} collective-permute-done((bf16[64,1664]{1,0:T(8,128)(2,1)S(1)}, bf16[64,1664]{1,0:T(8,128)(2,1)S(1)}, u32[]{:S(2)}, u32[]{:S(2)}) %collective-permute-start.10) | collective-permute-done | bytes 213024 | tf_op jit(solution)/shard_map/ppermute | solution.py:433
  44.6 0.5 collective-permute-start.16
  45.1 0.0 collective-permute-done.7.refs_9_
  45.1 0.0 collective-permute-start.13
  45.1 4.0 %collective-permute-done.9.refs_11_ = bf16[64,1664]{1,0:T(8,128)(2,1)S(1)} collective-permute-done((bf16[64,1664]{1,0:T(8,128)(2,1)S(1)}, bf16[64,1664]{1,0:T(8,128)(2,1)S(1)}, u32[]{:S(2)}, u32[]{:S(2)}) %collective-permute-start.9) | collective-permute-done | bytes 213024 | tf_op jit(solution)/shard_map/ppermute | solution.py:433
  49.1 0.0 collective-permute-start.12
  49.1 0.0 collective-permute-done.11.refs_13_
  49.1 0.0 collective-permute-start.18
  49.1 0.0 collective-permute-done.6.refs_8_
  49.1 0.6 collective-permute-start.15
  49.7 3.2 %collective-permute-done.16.refs_7_ = bf16[64,1664]{1,0:T(8,128)(2,1)S(1)} collective-permute-done((bf16[64,1664]{1,0:T(8,128)(2,1)S(1)}, bf16[64,1664]{1,0:T(8,128)(2,1)S(1)}, u32[]{:S(2)}, u32[]{:S(2)}) %collective-permute-start.16) | collective-permute-done | bytes 213024 | tf_op jit(solution)/shard_map/ppermute | solution.py:433
  52.9 0.0 collective-permute-start.17
  52.9 0.0 collective-permute-done.13.refs_15_
  52.9 0.0 collective-permute-start.23
  52.9 0.0 collective-permute-done.12.refs_14_
  52.9 2.0 %collective-permute-start.20 = (bf16[2,8,32,128]{3,2,1,0:T(8,128)(2,1)S(1)}, bf16[2,8,32,128]{3,2,1,0:T(8,128)(2,1)S(1)}, u32[]{:S(2)}, u32[]{:S(2)}) collective-permute-start(bf16[2,8,32,128]{3,2,1,0:T(8,128)(2,1)S(1)} %collective-permute-done.19.refs_11_), channel_id=1, source_target_pairs={{0,1},{1,0},{2,3},{3,2},{4,5},{5,4},{6,7},{7,6},{8,9},{9,8},{10,11... | collective-permute-start | bytes 393224 | tf_op jit(solution)/shard_map/ppermute | solution.py:433
  54.9 1.5 %gather.1.refs_4_ = bf16[256,1664]{1,0:T(8,128)(2,1)S(1)} custom-call(s32[32]{0:T(128)S(1)} %bitcast_add_fusion.refs_0_, s32[32]{0:T(128)S(1)} %collective-permute-done.refs_1_, s32[32]{0:T(128)S(1)} %collective-permute-done.1.refs_2_, s32[32]{0:T(128)S(1)} %collective-permute-done.2.refs_3_, bf16[64,1664]{1,0:T(8,128)(2,1)S(1)} %get-tuple-element.14.refs_4_, ...), custom_call_target="tpu_custom_call" | custom-call | tf_op jit(solution)/shard_map/gather/pallas_call | solution.py:279
  56.4 1.9 %collective-permute-done.18.refs_10_ = bf16[4,8,32,128]{3,2,1,0:T(8,128)(2,1)S(1)} collective-permute-done((bf16[4,8,32,128]{3,2,1,0:T(8,128)(2,1)S(1)}, bf16[4,8,32,128]{3,2,1,0:T(8,128)(2,1)S(1)}, u32[]{:S(2)}, u32[]{:S(2)}) %collective-permute-start.18) | collective-permute-done | bytes 262176 | tf_op jit(solution)/shard_map/ppermute | solution.py:433
  58.3 2.8 %collective-permute-done.23.refs_12_ = bf16[2,8,32,128]{3,2,1,0:T(8,128)(2,1)S(1)} collective-permute-done((bf16[2,8,32,128]{3,2,1,0:T(8,128)(2,1)S(1)}, bf16[2,8,32,128]{3,2,1,0:T(8,128)(2,1)S(1)}, u32[]{:S(2)}, u32[]{:S(2)}) %collective-permute-start.23) | collective-permute-done | bytes 131104 | tf_op jit(solution)/shard_map/ppermute | solution.py:433
  61.1 0.0 collective-permute-done.15.refs_6_
  61.1 0.0 collective-permute-done.17.refs_8_
  61.1 3.5 %convolve.3 = (f32[2,16,1536]{2,1,0:T(8,128)S(1)}, bf16[2,16,1536]{2,1,0:T(8,128)(2,1)S(1)}) custom-call(s32[32]{0:T(128)S(1)} %bitcast_add_fusion.refs_0_, s32[32]{0:T(128)S(1)} %collective-permute-done.refs_1_, s32[32]{0:T(128)S(1)} %collective-permute-done.1.refs_2_, s32[32]{0:T(128)S(1)} %collective-permute-done.2.refs_3_, ...), custom_call_target="tpu_custom_call" | custom-call | tf_op jit(solution)/shard_map/convolve/pallas_call | solution.py:375
  64.7 0.1 collective-permute-start.24
  64.7 0.0 collective-permute-done.20.refs_12_
  64.8 3.5 %convolve.2 = (f32[2,16,1536]{2,1,0:T(8,128)S(1)}, bf16[2,16,1536]{2,1,0:T(8,128)(2,1)S(1)}) custom-call(s32[32]{0:T(128)S(1)} %bitcast_add_fusion.refs_0_, s32[32]{0:T(128)S(1)} %collective-permute-done.refs_1_, s32[32]{0:T(128)S(1)} %collective-permute-done.1.refs_2_, s32[32]{0:T(128)S(1)} %collective-permute-done.2.refs_3_, ...), custom_call_target="tpu_custom_call" | custom-call | tf_op jit(solution)/shard_map/convolve/pallas_call | solution.py:375
  68.3 2.1 %collective-permute-start.21 = (bf16[2,16,1536]{2,1,0:T(8,128)(2,1)S(1)}, bf16[2,16,1536]{2,1,0:T(8,128)(2,1)S(1)}, u32[]{:S(2)}, u32[]{:S(2)}) collective-permute-start(bf16[2,16,1536]{2,1,0:T(8,128)(2,1)S(1)} %get-tuple-element.19), channel_id=1, source_target_pairs={{0,1},{1,0},{2,3},{3,2},{4,5},{5,4},{6,7},{7,6},{8,9},{9,8},{10,11... | collective-permute-start | bytes 294920 | tf_op jit(solution)/shard_map/ppermute | solution.py:433
  70.4 0.0 collective-permute-done.24.got_ref
  70.4 0.8 %assemble.2.refs_0_ = f32[4,3,16,1024]{3,2,1,0:T(8,128)} custom-call(f32[2,16,1536]{2,1,0:T(8,128)S(1)} %get-tuple-element.21.own_ref, bf16[2,16,1536]{2,1,0:T(8,128)(2,1)S(1)} %collective-permute-done.24.got_ref), custom_call_target="tpu_custom_call" | custom-call | tf_op jit(solution)/shard_map/assemble/pallas_call | solution.py:420
  71.1 1.9 %collective-permute-done.21.got_ref = bf16[2,16,1536]{2,1,0:T(8,128)(2,1)S(1)} collective-permute-done((bf16[2,16,1536]{2,1,0:T(8,128)(2,1)S(1)}, bf16[2,16,1536]{2,1,0:T(8,128)(2,1)S(1)}, u32[]{:S(2)}, u32[]{:S(2)}) %collective-permute-start.21) | collective-permute-done | bytes 98336 | tf_op jit(solution)/shard_map/ppermute | solution.py:433
  73.0 0.8 %assemble.3 = f32[4,3,16,1024]{3,2,1,0:T(8,128)} custom-call(f32[2,16,1536]{2,1,0:T(8,128)S(1)} %get-tuple-element.18.own_ref, bf16[2,16,1536]{2,1,0:T(8,128)(2,1)S(1)} %collective-permute-done.21.got_ref, f32[4,3,16,1024]{3,2,1,0:T(8,128)} %assemble.2.refs_0_), custom_call_target="tpu_custom_call", output_to_operand_aliasing={{}: (2, {})} | custom-call | tf_op jit(solution)/shard_map/assemble/pallas_call | solution.py:420
  (3 shorter events, 0.0 us)
Async XLA Ops:
  0.0 10.5 %copy-start.3 = (s32[32,1]{0,1:T(1,128)S(1)}, s32[32,1]{0,1:T(1,128)}, u32[]{:S(2)}) copy-start(s32[32,1]{0,1:T(1,128)} %param.7) | copy-start | bytes 388
  0.0 10.5 %copy-start.2 = (s32[32]{0:T(128)S(1)}, s32[32]{0:T(128)}, u32[]{:S(2)}) copy-start(s32[32]{0:T(128)} %param.8) | copy-start | bytes 388
  0.7 1.7 %copy-start = (bf16[64,6,3,1024]{3,0,2,1:T(8,128)(2,1)S(1)}, bf16[64,6,3,1024]{3,0,2,1:T(8,128)(2,1)}, u32[]{:S(2)}) copy-start(bf16[64,6,3,1024]{3,0,2,1:T(8,128)(2,1)} %param.5) | copy-start | bytes 7077892
  2.4 5.1 %copy-start.1 = (bf16[32,64,128]{2,1,0:T(8,128)(2,1)S(1)}, bf16[32,64,128]{2,1,0:T(8,128)(2,1)}, u32[]{:S(2)}) copy-start(bf16[32,64,128]{2,1,0:T(8,128)(2,1)} %slip_ref.1) | copy-start | bytes 1572868
  3.3 33.1 %collective-permute-start.4 = (bf16[64,1664]{1,0:T(8,128)(2,1)S(1)}, bf16[64,1664]{1,0:T(8,128)(2,1)S(1)}, u32[]{:S(2)}, u32[]{:S(2)}) collective-permute-start(bf16[64,1664]{1,0:T(8,128)(2,1)S(1)} %get-tuple-element.14.refs_4_), channel_id=1, source_target_pairs={{0,2},{1,3},{2,0},{3,1},{4,6},{5,7},{6,4},{7,5},{8,10},{9,11},{10,... | collective-permute-start | bytes 638984 | tf_op jit(solution)/shard_map/ppermute | solution.py:433
  10.4 23.6 %collective-permute-start.22 = (bf16[2,8,32,128]{3,2,1,0:T(8,128)(2,1)S(1)}, bf16[2,8,32,128]{3,2,1,0:T(8,128)(2,1)S(1)}, u32[]{:S(2)}, u32[]{:S(2)}) collective-permute-start(bf16[2,8,32,128]{3,2,1,0:T(8,128)(2,1)S(1)} %get-tuple-element.20), channel_id=1, source_target_pairs={{0,2},{1,3},{2,0},{3,1},{4,6},{5,7},{6,4},{7,5},{8,10},{9,11},{10,... | collective-permute-start | bytes 393224 | tf_op jit(solution)/shard_map/ppermute | solution.py:433
  10.5 5.0 %collective-permute-start = (s32[32]{0:T(128)S(1)}, s32[32]{0:T(128)S(1)}, u32[]{:S(2)}, u32[]{:S(2)}) collective-permute-start(s32[32]{0:T(128)S(1)} %bitcast_add_fusion.refs_0_), channel_id=1, source_target_pairs={{0,1},{1,0},{2,3},{3,2},{4,5},{5,4},{6,7},{7,6},{8,9},{9,8},{10,11... | collective-permute-start | bytes 392 | tf_op jit(solution)/shard_map/ppermute | solution.py:433
  12.4 14.4 %collective-permute-start.1 = (s32[32]{0:T(128)S(1)}, s32[32]{0:T(128)S(1)}, u32[]{:S(2)}, u32[]{:S(2)}) collective-permute-start(s32[32]{0:T(128)S(1)} %bitcast_add_fusion.refs_0_), channel_id=1, source_target_pairs={{0,2},{1,3},{2,0},{3,1},{4,6},{5,7},{6,4},{7,5},{8,10},{9,11},{10,... | collective-permute-start | bytes 392 | tf_op jit(solution)/shard_map/ppermute | solution.py:433
  15.0 22.0 %collective-permute-start.3 = (bf16[64,1664]{1,0:T(8,128)(2,1)S(1)}, bf16[64,1664]{1,0:T(8,128)(2,1)S(1)}, u32[]{:S(2)}, u32[]{:S(2)}) collective-permute-start(bf16[64,1664]{1,0:T(8,128)(2,1)S(1)} %get-tuple-element.15), channel_id=1, source_target_pairs={{0,1},{1,0},{2,3},{3,2},{4,5},{5,4},{6,7},{7,6},{8,9},{9,8},{10,11... | collective-permute-start | bytes 638984 | tf_op jit(solution)/shard_map/ppermute | solution.py:433
  15.5 18.5 %collective-permute-start.19 = (bf16[2,8,32,128]{3,2,1,0:T(8,128)(2,1)S(1)}, bf16[2,8,32,128]{3,2,1,0:T(8,128)(2,1)S(1)}, u32[]{:S(2)}, u32[]{:S(2)}) collective-permute-start(bf16[2,8,32,128]{3,2,1,0:T(8,128)(2,1)S(1)} %get-tuple-element.17), channel_id=1, source_target_pairs={{0,2},{1,3},{2,0},{3,1},{4,6},{5,7},{6,4},{7,5},{8,10},{9,11},{10,... | collective-permute-start | bytes 393224 | tf_op jit(solution)/shard_map/ppermute | solution.py:433
  26.8 5.4 %collective-permute-start.2 = (s32[32]{0:T(128)S(1)}, s32[32]{0:T(128)S(1)}, u32[]{:S(2)}, u32[]{:S(2)}) collective-permute-start(s32[32]{0:T(128)S(1)} %bitcast_add_fusion.refs_0_), channel_id=1, source_target_pairs={{0,3},{1,2},{2,1},{3,0},{4,7},{5,6},{6,5},{7,4},{8,11},{9,10},{10,... | collective-permute-start | bytes 392 | tf_op jit(solution)/shard_map/ppermute | solution.py:433
  32.2 5.8 %collective-permute-start.8 = (bf16[64,1664]{1,0:T(8,128)(2,1)S(1)}, bf16[64,1664]{1,0:T(8,128)(2,1)S(1)}, u32[]{:S(2)}, u32[]{:S(2)}) collective-permute-start(bf16[64,1664]{1,0:T(8,128)(2,1)S(1)} %get-tuple-element.14.refs_4_), channel_id=1, source_target_pairs={{0,8},{4,12},{8,0},{12,4},{1,9},{5,13},{9,1},{13,5},{2,10},{6,14},... | collective-permute-start | bytes 638984 | tf_op jit(solution)/shard_map/ppermute | solution.py:433
  34.0 5.9 %collective-permute-start.5 = (bf16[64,1664]{1,0:T(8,128)(2,1)S(1)}, bf16[64,1664]{1,0:T(8,128)(2,1)S(1)}, u32[]{:S(2)}, u32[]{:S(2)}) collective-permute-start(bf16[64,1664]{1,0:T(8,128)(2,1)S(1)} %get-tuple-element.14.refs_4_), channel_id=1, source_target_pairs={{0,4},{4,0},{8,12},{12,8},{1,5},{5,1},{9,13},{13,9},{2,6},{6,2},{1... | collective-permute-start | bytes 638984 | tf_op jit(solution)/shard_map/ppermute | solution.py:433
  34.0 9.5 %collective-permute-start.14 = (bf16[64,1664]{1,0:T(8,128)(2,1)S(1)}, bf16[64,1664]{1,0:T(8,128)(2,1)S(1)}, u32[]{:S(2)}, u32[]{:S(2)}) collective-permute-start(bf16[64,1664]{1,0:T(8,128)(2,1)S(1)} %get-tuple-element.15), channel_id=1, source_target_pairs={{0,3},{1,2},{2,1},{3,0},{4,7},{5,6},{6,5},{7,4},{8,11},{9,10},{10,... | collective-permute-start | bytes 638984 | tf_op jit(solution)/shard_map/ppermute | solution.py:433
  36.4 8.1 %collective-permute-start.10 = (bf16[64,1664]{1,0:T(8,128)(2,1)S(1)}, bf16[64,1664]{1,0:T(8,128)(2,1)S(1)}, u32[]{:S(2)}, u32[]{:S(2)}) collective-permute-start(bf16[64,1664]{1,0:T(8,128)(2,1)S(1)} %collective-permute-done.4.refs_6_), channel_id=1, source_target_pairs={{0,8},{4,12},{8,0},{12,4},{1,9},{5,13},{9,1},{13,5},{2,10},{6,14},... | collective-permute-start | bytes 638984 | tf_op jit(solution)/shard_map/ppermute | solution.py:433
  37.0 8.1 %collective-permute-start.7 = (bf16[64,1664]{1,0:T(8,128)(2,1)S(1)}, bf16[64,1664]{1,0:T(8,128)(2,1)S(1)}, u32[]{:S(2)}, u32[]{:S(2)}) collective-permute-start(bf16[64,1664]{1,0:T(8,128)(2,1)S(1)} %collective-permute-done.4.refs_6_), channel_id=1, source_target_pairs={{0,4},{4,0},{8,12},{12,8},{1,5},{5,1},{9,13},{13,9},{2,6},{6,2},{1... | collective-permute-start | bytes 638984 | tf_op jit(solution)/shard_map/ppermute | solution.py:433
  38.0 11.1 %collective-permute-start.9 = (bf16[64,1664]{1,0:T(8,128)(2,1)S(1)}, bf16[64,1664]{1,0:T(8,128)(2,1)S(1)}, u32[]{:S(2)}, u32[]{:S(2)}) collective-permute-start(bf16[64,1664]{1,0:T(8,128)(2,1)S(1)} %collective-permute-done.3.refs_5_), channel_id=1, source_target_pairs={{0,8},{4,12},{8,0},{12,4},{1,9},{5,13},{9,1},{13,5},{2,10},{6,14},... | collective-permute-start | bytes 638984 | tf_op jit(solution)/shard_map/ppermute | solution.py:433
  39.9 9.2 %collective-permute-start.11 = (bf16[64,1664]{1,0:T(8,128)(2,1)S(1)}, bf16[64,1664]{1,0:T(8,128)(2,1)S(1)}, u32[]{:S(2)}, u32[]{:S(2)}) collective-permute-start(bf16[64,1664]{1,0:T(8,128)(2,1)S(1)} %collective-permute-done.8.refs_10_), channel_id=1, source_target_pairs={{0,4},{4,0},{8,12},{12,8},{1,5},{5,1},{9,13},{13,9},{2,6},{6,2},{1... | collective-permute-start | bytes 638984 | tf_op jit(solution)/shard_map/ppermute | solution.py:433
  43.4 5.7 %collective-permute-start.6 = (bf16[64,1664]{1,0:T(8,128)(2,1)S(1)}, bf16[64,1664]{1,0:T(8,128)(2,1)S(1)}, u32[]{:S(2)}, u32[]{:S(2)}) collective-permute-start(bf16[64,1664]{1,0:T(8,128)(2,1)S(1)} %collective-permute-done.3.refs_5_), channel_id=1, source_target_pairs={{0,4},{4,0},{8,12},{12,8},{1,5},{5,1},{9,13},{13,9},{2,6},{6,2},{1... | collective-permute-start | bytes 638984 | tf_op jit(solution)/shard_map/ppermute | solution.py:433
  44.6 8.3 %collective-permute-start.16 = (bf16[64,1664]{1,0:T(8,128)(2,1)S(1)}, bf16[64,1664]{1,0:T(8,128)(2,1)S(1)}, u32[]{:S(2)}, u32[]{:S(2)}) collective-permute-start(bf16[64,1664]{1,0:T(8,128)(2,1)S(1)} %collective-permute-done.14.refs_5_), channel_id=1, source_target_pairs={{0,8},{4,12},{8,0},{12,4},{1,9},{5,13},{9,1},{13,5},{2,10},{6,14},... | collective-permute-start | bytes 638984 | tf_op jit(solution)/shard_map/ppermute | solution.py:433
  45.1 7.8 %collective-permute-start.13 = (bf16[64,1664]{1,0:T(8,128)(2,1)S(1)}, bf16[64,1664]{1,0:T(8,128)(2,1)S(1)}, u32[]{:S(2)}, u32[]{:S(2)}) collective-permute-start(bf16[64,1664]{1,0:T(8,128)(2,1)S(1)} %collective-permute-done.10.refs_12_), channel_id=1, source_target_pairs={{0,4},{4,0},{8,12},{12,8},{1,5},{5,1},{9,13},{13,9},{2,6},{6,2},{1... | collective-permute-start | bytes 638984 | tf_op jit(solution)/shard_map/ppermute | solution.py:433
  49.1 3.8 %collective-permute-start.12 = (bf16[64,1664]{1,0:T(8,128)(2,1)S(1)}, bf16[64,1664]{1,0:T(8,128)(2,1)S(1)}, u32[]{:S(2)}, u32[]{:S(2)}) collective-permute-start(bf16[64,1664]{1,0:T(8,128)(2,1)S(1)} %collective-permute-done.9.refs_11_), channel_id=1, source_target_pairs={{0,4},{4,0},{8,12},{12,8},{1,5},{5,1},{9,13},{13,9},{2,6},{6,2},{1... | collective-permute-start | bytes 638984 | tf_op jit(solution)/shard_map/ppermute | solution.py:433
  49.1 9.2 %collective-permute-start.18 = (bf16[4,8,32,128]{3,2,1,0:T(8,128)(2,1)S(1)}, bf16[4,8,32,128]{3,2,1,0:T(8,128)(2,1)S(1)}, u32[]{:S(2)}, u32[]{:S(2)}) collective-permute-start(bf16[4,8,32,128]{3,2,1,0:T(8,128)(2,1)S(1)} %get-tuple-element.16.refs_9_), channel_id=1, source_target_pairs={{0,1},{1,0},{2,3},{3,2},{4,5},{5,4},{6,7},{7,6},{8,9},{9,8},{10,11... | collective-permute-start | bytes 786440 | tf_op jit(solution)/shard_map/ppermute | solution.py:433
  49.1 12.0 %collective-permute-start.15 = (bf16[64,1664]{1,0:T(8,128)(2,1)S(1)}, bf16[64,1664]{1,0:T(8,128)(2,1)S(1)}, u32[]{:S(2)}, u32[]{:S(2)}) collective-permute-start(bf16[64,1664]{1,0:T(8,128)(2,1)S(1)} %collective-permute-done.14.refs_5_), channel_id=1, source_target_pairs={{0,4},{4,0},{8,12},{12,8},{1,5},{5,1},{9,13},{13,9},{2,6},{6,2},{1... | collective-permute-start | bytes 638984 | tf_op jit(solution)/shard_map/ppermute | solution.py:433
  52.9 8.2 %collective-permute-start.17 = (bf16[64,1664]{1,0:T(8,128)(2,1)S(1)}, bf16[64,1664]{1,0:T(8,128)(2,1)S(1)}, u32[]{:S(2)}, u32[]{:S(2)}) collective-permute-start(bf16[64,1664]{1,0:T(8,128)(2,1)S(1)} %collective-permute-done.16.refs_7_), channel_id=1, source_target_pairs={{0,4},{4,0},{8,12},{12,8},{1,5},{5,1},{9,13},{13,9},{2,6},{6,2},{1... | collective-permute-start | bytes 638984 | tf_op jit(solution)/shard_map/ppermute | solution.py:433
  52.9 8.2 %collective-permute-start.23 = (bf16[2,8,32,128]{3,2,1,0:T(8,128)(2,1)S(1)}, bf16[2,8,32,128]{3,2,1,0:T(8,128)(2,1)S(1)}, u32[]{:S(2)}, u32[]{:S(2)}) collective-permute-start(bf16[2,8,32,128]{3,2,1,0:T(8,128)(2,1)S(1)} %collective-permute-done.22.refs_11_), channel_id=1, source_target_pairs={{0,1},{1,0},{2,3},{3,2},{4,5},{5,4},{6,7},{7,6},{8,9},{9,8},{10,11... | collective-permute-start | bytes 393224 | tf_op jit(solution)/shard_map/ppermute | solution.py:433
  52.9 11.8 %collective-permute-start.20 = (bf16[2,8,32,128]{3,2,1,0:T(8,128)(2,1)S(1)}, bf16[2,8,32,128]{3,2,1,0:T(8,128)(2,1)S(1)}, u32[]{:S(2)}, u32[]{:S(2)}) collective-permute-start(bf16[2,8,32,128]{3,2,1,0:T(8,128)(2,1)S(1)} %collective-permute-done.19.refs_11_), channel_id=1, source_target_pairs={{0,1},{1,0},{2,3},{3,2},{4,5},{5,4},{6,7},{7,6},{8,9},{9,8},{10,11... | collective-permute-start | bytes 393224 | tf_op jit(solution)/shard_map/ppermute | solution.py:433
  64.7 5.7 %collective-permute-start.24 = (bf16[2,16,1536]{2,1,0:T(8,128)(2,1)S(1)}, bf16[2,16,1536]{2,1,0:T(8,128)(2,1)S(1)}, u32[]{:S(2)}, u32[]{:S(2)}) collective-permute-start(bf16[2,16,1536]{2,1,0:T(8,128)(2,1)S(1)} %get-tuple-element.22), channel_id=1, source_target_pairs={{0,1},{1,0},{2,3},{3,2},{4,5},{5,4},{6,7},{7,6},{8,9},{9,8},{10,11... | collective-permute-start | bytes 294920 | tf_op jit(solution)/shard_map/ppermute | solution.py:433
  68.3 4.7 %collective-permute-start.21 = (bf16[2,16,1536]{2,1,0:T(8,128)(2,1)S(1)}, bf16[2,16,1536]{2,1,0:T(8,128)(2,1)S(1)}, u32[]{:S(2)}, u32[]{:S(2)}) collective-permute-start(bf16[2,16,1536]{2,1,0:T(8,128)(2,1)S(1)} %get-tuple-element.19), channel_id=1, source_target_pairs={{0,1},{1,0},{2,3},{3,2},{4,5},{5,4},{6,7},{7,6},{8,9},{9,8},{10,11... | collective-permute-start | bytes 294920 | tf_op jit(solution)/shard_map/ppermute | solution.py:433
